TPU v7x, 8 devices: a whole 2x2x1 slice. The times are simulated.
8 devices in a mesh: rep: 1 (over z), kv: 8 (over y, x, core).
Axes of the slice: x: 2, y: 2, z: 1, core: 2. Of those that a mesh axis runs over, the one named last changes fastest.
Arguments:
- embeds: bfloat16 [2, 192, 4096], P(None, ('rep', 'kv'))
- w_query: bfloat16 [2, 4096, 4096], replicated
- w_key: bfloat16 [2, 4096, 1024], replicated
- w_value: bfloat16 [2, 4096, 1024], replicated
- w_out: bfloat16 [2, 4096, 4096], replicated
- w_up: bfloat16 [2, 4096, 14336], replicated
- w_down: bfloat16 [2, 14336, 4096], replicated
- k_pool: bfloat16 [1152, 2, 32, 8, 128], P(('rep', 'kv'))
- v_pool: bfloat16 [1152, 2, 32, 8, 128], P(('rep', 'kv'))
- old_table: int32 [192, 4], P('rep')
- new_table: int32 [192, 4], P('rep')
- seq_len: int32 [192], P('rep')
- finished: int32 [192], P('rep')
- mig_src: int32 [384], P('rep')
- mig_dst: int32 [384], P('rep')
Outputs:
- output 1: bfloat16 [2, 192, 4096], P(None, ('rep', 'kv'))
- output 2: bfloat16 [1152, 2, 32, 8, 128], P(('rep', 'kv'))
- output 3: bfloat16 [1152, 2, 32, 8, 128], P(('rep', 'kv'))
All inputs are finite; a program needn't handle non-finite values.
Results may differ from a plain program's by a relative error of at most 0.0164136.
Values are sent between devices in bfloat16 or wider.
A program may use at most 2.75 GiB of HBM per device.

v0:
```python
import jax
import jax.numpy as jnp
from jax import lax
from jax.sharding import PartitionSpec as P


def solution(mesh):
    groups = mesh.shape['kv']
    rows_spec = P(None, ('rep', 'kv'), None)
    pool_spec = P(('rep', 'kv'))
    table_spec = P('rep', None)
    vec_spec = P('rep')
    full_spec = P()

    def device_fn(embeds, w_query, w_key, w_value, w_out, w_up, w_down, k_pool, v_pool, old_table, new_table, seq_len, finished, mig_src, mig_dst):
        my_dev = lax.axis_index('kv')
        slots_dev, n_layers, page_size, kv_heads, head_dim = k_pool.shape
        seq_dev = embeds.shape[1]
        n_batch, pages_seq = old_table.shape
        q_width = w_query.shape[2]
        kv_width = kv_heads * head_dim
        rep_factor = q_width // kv_width
        n_mig = mig_src.shape[0]
        pair_cap = 4 * n_mig // (groups * groups)
        score_scale = head_dim ** -0.5
        slot_base = my_dev * slots_dev
        seq_ids = jnp.arange(n_batch, dtype=jnp.int32)
        active = finished == 0
        len_next = seq_len + 1
        home_done = lax.dynamic_slice(finished, (my_dev * seq_dev,), (seq_dev,))

        def slot_maps(table, only_active):
            local_slot = table - slot_base
            keep_mask = (local_slot >= 0) & (local_slot < slots_dev)
            if only_active:
                keep_mask = keep_mask & active[:, None]
            target = jnp.where(keep_mask, local_slot, slots_dev).reshape(-1)
            slot_owner = jnp.full((slots_dev,), n_batch, jnp.int32).at[target].set(jnp.repeat(seq_ids, pages_seq), mode='drop')
            slot_page = jnp.zeros((slots_dev,), jnp.int32).at[target].set(jnp.tile(jnp.arange(pages_seq, dtype=jnp.int32), n_batch), mode='drop')
            return slot_owner, slot_page

        def project_all(hidden, layer_idx):
            query_loc = jnp.dot(hidden, w_query[layer_idx], preferred_element_type=jnp.float32).astype(jnp.bfloat16)
            k_loc = jnp.dot(hidden, w_key[layer_idx], preferred_element_type=jnp.float32).astype(jnp.bfloat16)
            v_loc = jnp.dot(hidden, w_value[layer_idx], preferred_element_type=jnp.float32).astype(jnp.bfloat16)
            packed = jnp.concatenate([query_loc, k_loc, v_loc], axis=1)
            gathered = lax.all_gather(packed, 'kv', axis=0, tiled=True)
            query_rows = gathered[:, :q_width]
            k_new = gathered[:, q_width:q_width + kv_width].reshape(n_batch, kv_heads, head_dim)
            v_new = gathered[:, q_width + kv_width:].reshape(n_batch, kv_heads, head_dim)
            return query_rows, k_new, v_new

        def write_new(k_layer, v_layer, k_new, v_new, table, lengths, only_active):
            page_now = lengths // page_size
            local_slot = jnp.take_along_axis(table, page_now[:, None], axis=1)[:, 0] - slot_base
            keep_mask = (local_slot >= 0) & (local_slot < slots_dev)
            if only_active:
                keep_mask = keep_mask & active
            write_rows = jnp.where(keep_mask, local_slot, slots_dev)
            offset = lengths % page_size
            return k_layer.at[write_rows, offset].set(k_new, mode='drop'), v_layer.at[write_rows, offset].set(v_new, mode='drop')

        def to_home(values):
            return lax.all_to_all(values, 'kv', 0, 0, tiled=True)

        def attend(query_rows, k_layer, v_layer, slot_owner, slot_page, lengths):
            q_slot = jnp.take(query_rows, slot_owner, axis=0, mode='clip').reshape(slots_dev, kv_heads, rep_factor, head_dim)
            scores = jnp.einsum('sgrd,spgd->sgrp', q_slot, k_layer, preferred_element_type=jnp.float32) * score_scale
            len_slot = jnp.take(lengths, slot_owner, mode='clip')
            positions = slot_page[:, None] * page_size + jnp.arange(page_size)[None, :]
            valid_pos = (positions <= len_slot[:, None]) & (slot_owner < n_batch)[:, None]
            scores = jnp.where(valid_pos[:, None, None, :], scores, -1e30)
            slot_max = scores.max(axis=-1)
            exp_scores = jnp.exp(scores - slot_max[..., None])
            slot_sum = exp_scores.sum(axis=-1)
            slot_out = jnp.einsum('sgrp,spgd->sgrd', exp_scores.astype(jnp.bfloat16), v_layer, preferred_element_type=jnp.float32)
            seq_max = jnp.full((n_batch, kv_heads, rep_factor), -jnp.inf, jnp.float32).at[slot_owner].max(slot_max, mode='drop')
            factor = jnp.exp(slot_max - jnp.take(seq_max, slot_owner, axis=0, mode='clip'))
            seq_sum = jax.ops.segment_sum(slot_sum * factor, slot_owner, num_segments=n_batch)
            seq_out = jax.ops.segment_sum(slot_out * factor[..., None], slot_owner, num_segments=n_batch)
            stats_home = to_home(jnp.stack([seq_max, seq_sum], axis=1)).reshape(groups, seq_dev, 2, kv_heads, rep_factor)
            out_home = to_home(seq_out).reshape(groups, seq_dev, kv_heads, rep_factor, head_dim)
            top_max = stats_home[:, :, 0].max(axis=0)
            top_max = jnp.where(jnp.isfinite(top_max), top_max, 0.0)
            weight_home = jnp.exp(stats_home[:, :, 0] - top_max)
            total_sum = (stats_home[:, :, 1] * weight_home).sum(axis=0)
            acc_home = (out_home * weight_home[..., None]).sum(axis=0)
            result = acc_home / jnp.where(total_sum > 0, total_sum, 1.0)[..., None]
            return result.astype(jnp.bfloat16).reshape(seq_dev, q_width)

        def finish_block(hidden, attn_rows, layer_idx):
            mixed_rows = (hidden.astype(jnp.float32) + jnp.dot(attn_rows, w_out[layer_idx], preferred_element_type=jnp.float32)).astype(jnp.bfloat16)
            inner_act = jax.nn.gelu(jnp.dot(mixed_rows, w_up[layer_idx], preferred_element_type=jnp.float32)).astype(jnp.bfloat16)
            return (mixed_rows.astype(jnp.float32) + jnp.dot(inner_act, w_down[layer_idx], preferred_element_type=jnp.float32)).astype(jnp.bfloat16)

        src_dev = mig_src // slots_dev
        dst_dev = mig_dst // slots_dev
        pair_key = src_dev * groups + dst_dev
        order_idx = jnp.argsort(pair_key, stable=True)
        sorted_key = pair_key[order_idx]
        first_pos = jnp.searchsorted(sorted_key, sorted_key, side='left')
        pair_rank = jnp.zeros((n_mig,), jnp.int32).at[order_idx].set(jnp.arange(n_mig, dtype=jnp.int32) - first_pos)
        send_pos = jnp.where(src_dev == my_dev, dst_dev * pair_cap + pair_rank, groups * pair_cap)
        send_slot = jnp.zeros((groups * pair_cap,), jnp.int32).at[send_pos].set(mig_src - slot_base, mode='drop')
        recv_pos = jnp.where(dst_dev == my_dev, src_dev * pair_cap + pair_rank, groups * pair_cap)
        recv_slot = jnp.full((groups * pair_cap,), slots_dev, jnp.int32).at[recv_pos].set(mig_dst - slot_base, mode='drop')

        def migrate(k_layer, v_layer):
            outgoing = jnp.stack([k_layer[send_slot], v_layer[send_slot]], axis=1)
            incoming = lax.all_to_all(outgoing, 'kv', 0, 0, tiled=True)
            return k_layer.at[recv_slot].set(incoming[:, 0], mode='drop'), v_layer.at[recv_slot].set(incoming[:, 1], mode='drop')

        old_owner, old_page = slot_maps(old_table, False)
        new_owner, new_page = slot_maps(new_table, True)
        hid_zero = embeds[0]
        hid_one = embeds[1]
        k_layers = []
        v_layers = []
        for layer_idx in range(n_layers):
            k_layer = k_pool[:, layer_idx]
            v_layer = v_pool[:, layer_idx]
            query_rows, k_new, v_new = project_all(hid_zero, layer_idx)
            k_layer, v_layer = write_new(k_layer, v_layer, k_new, v_new, old_table, seq_len, False)
            hid_zero = finish_block(hid_zero, attend(query_rows, k_layer, v_layer, old_owner, old_page, seq_len), layer_idx)
            k_layer, v_layer = migrate(k_layer, v_layer)
            query_rows, k_new, v_new = project_all(hid_one, layer_idx)
            k_layer, v_layer = write_new(k_layer, v_layer, k_new, v_new, new_table, len_next, True)
            hid_one = finish_block(hid_one, attend(query_rows, k_layer, v_layer, new_owner, new_page, len_next), layer_idx)
            k_layers.append(k_layer)
            v_layers.append(v_layer)
        hid_one = jnp.where(home_done[:, None] == 0, hid_one, jnp.zeros_like(hid_one))
        return jnp.stack([hid_zero, hid_one]), jnp.stack(k_layers, axis=1), jnp.stack(v_layers, axis=1)

    in_specs = (rows_spec, full_spec, full_spec, full_spec, full_spec, full_spec, full_spec, pool_spec, pool_spec, table_spec, table_spec, vec_spec, vec_spec, vec_spec, vec_spec)
    return jax.shard_map(device_fn, mesh=mesh, in_specs=in_specs, out_specs=(rows_spec, pool_spec, pool_spec), check_vma=False)
```

profile of v0, /device:TPU:0, one launch (start us, length us, event | category | flops | bytes accessed | tf_op | source)
XLA Modules:
  0.0 1711.4 jit_solution(18394631168738583200)
XLA Ops:
  82.7 22.0 %scatter_fusion = bf16[144,32,8,128]{3,2,1,0:T(8,128)(2,1)} fusion(bf16[144,32,8,128]{3,2,1,0:T(8,128)(2,1)} %get-tuple-element.122, s32[192]{0:T(256)S(1)} %bitcast.399, bf16[192,8,128]{2,1,0:T(8,128)(2,1)S(1)} %bitcast.436), kind=kCustom, calls=%fused_computation.20 | custom fusion | bytes 1181184 | tf_op jit(solution)/shard_map/scatter | solution.py:61
  139.5 21.4 %scatter_fusion.1 = bf16[144,32,8,128]{3,2,1,0:T(8,128)(2,1)} fusion(bf16[144,32,8,128]{3,2,1,0:T(8,128)(2,1)} %get-tuple-element.123, s32[192]{0:T(256)S(1)} %bitcast.400, bf16[192,8,128]{2,1,0:T(8,128)(2,1)S(1)} %bitcast.433), kind=kCustom, calls=%fused_computation.21 | custom fusion | bytes 1181184 | tf_op jit(solution)/shard_map/scatter | solution.py:61
  195.7 31.6 %all-to-all-done = f32[192,8,4,128]{3,1,2,0:T(8,128)S(1)} async-done(((f32[192,8,4,128]{3,1,2,0:T(8,128)}), f32[192,8,4,128]{3,1,2,0:T(8,128)S(1)}, u32[]{:S(2)}, u32[]{:S(2)}) %all-to-all-start) | async-done | bytes 3145760 | tf_op jit(solution)/shard_map/all_to_all | solution.py:64
  241.7 37.7 %fusion.182.clone.2 = bf16[24,14336]{1,0:T(8,128)(2,1)S(1)} fusion(bf16[24,4096]{1,0:T(8,128)(2,1)S(1)} %fusion.133, bf16[2,4096,14336]{2,1,0:T(8,128)(2,1)} %param.24), kind=kOutput, calls=%fused_computation.207.clone.clone.clone | convolution fusion | flops 2821668864 | bytes 118325248 | tf_op jit(solution)/shard_map/dot_general | solution.py:93
  279.4 37.6 %fusion.121 = bf16[24,4096]{1,0:T(8,128)(2,1)S(1)} fusion(bf16[2,14336,4096]{2,1,0:T(8,128)(2,1)} %param.25, bf16[24,4096]{1,0:T(8,128)(2,1)S(1)} %fusion.133, bf16[24,14336]{1,0:T(8,128)(2,1)S(1)} %fusion.182.clone.2), kind=kOutput, calls=%fused_computation.164 | convolution fusion | flops 2818867200 | bytes 118521856 | tf_op jit(solution)/shard_map/dot_general | solution.py:94
  367.9 22.2 %scatter_fusion.5 = bf16[144,32,8,128]{3,2,1,0:T(8,128)(2,1)} fusion(bf16[144,32,8,128]{3,2,1,0:T(8,128)(2,1)} %get-tuple-element.121, s32[192]{0:T(256)S(1)} %bitcast.401, bf16[192,8,128]{2,1,0:T(8,128)(2,1)S(1)} %bitcast.435), kind=kCustom, calls=%fused_computation.25 | custom fusion | bytes 1181184 | tf_op jit(solution)/shard_map/scatter | solution.py:61
  423.1 21.8 %scatter_fusion.6 = bf16[144,32,8,128]{3,2,1,0:T(8,128)(2,1)} fusion(bf16[144,32,8,128]{3,2,1,0:T(8,128)(2,1)} %get-tuple-element.124, s32[192]{0:T(256)S(1)} %bitcast.402, bf16[192,8,128]{2,1,0:T(8,128)(2,1)S(1)} %bitcast.432), kind=kCustom, calls=%fused_computation.26 | custom fusion | bytes 1181184 | tf_op jit(solution)/shard_map/scatter | solution.py:61
  474.1 26.0 %while.25 = (s32[]{:T(128)}, u32[384]{0:T(512)S(1)}, u32[384]{0:T(512)S(1)}, s32[384]{0:T(512)S(1)}, s32[]{:T(128)}, /*index=5*/s32[]{:T(128)}, s32[]{}) while((s32[]{:T(128)}, u32[384]{0:T(512)S(1)}, u32[384]{0:T(512)S(1)}, s32[384]{0:T(512)S(1)}, s32[]{:T(128)}, /*index=5*/s32[]{:T(128)}, s32[]{}) %tuple.82), condition=%wide.region_26.28_spmd.clone, body=%wide.region_25.27_spmd.clone.sunk | while | flops 7940 | bytes 31077 | solution.py:101
  530.2 20.5 %pad_maximum_fusion = bf16[192,2,32,8,128]{4,3,2,1,0:T(8,128)(2,1)} fusion(bf16[192,1,32,8,128]{4,3,2,1,0:T(8,128)(2,1)} %bitcast.406, bf16[192,1,32,8,128]{4,3,2,1,0:T(8,128)(2,1)} %bitcast.405), kind=kLoop, calls=%fused_computation.101 | loop fusion | flops 12582912 | bytes 50331648 | tf_op jit(solution)/shard_map/stack | solution.py:109
  594.6 118.7 %all-gather.9.cloned.1.call-done = bf16[192,6144]{1,0:T(8,128)(2,1)} async-done(((bf16[24,6144]{1,0:T(8,128)(2,1)}), bf16[192,6144]{1,0:T(8,128)(2,1)}) %all-gather.9.cloned.1.call-update) | async-done | bytes 2359312 | tf_op jit(solution)/shard_map/all_gather | solution.py:47
  742.2 20.7 %pad_maximum_fusion.1 = bf16[192,2,32,8,128]{4,3,2,1,0:T(8,128)(2,1)} fusion(bf16[192,1,32,8,128]{4,3,2,1,0:T(8,128)(2,1)} %bitcast.404, bf16[192,1,32,8,128]{4,3,2,1,0:T(8,128)(2,1)} %bitcast.403), kind=kLoop, calls=%fused_computation.102 | loop fusion | flops 12582912 | bytes 50331648 | tf_op jit(solution)/shard_map/stack | solution.py:109
  772.3 68.7 %all-to-all-done.4 = bf16[192,2,32,8,128]{4,3,2,1,0:T(8,128)(2,1)} async-done(((bf16[192,2,32,8,128]{4,3,2,1,0:T(8,128)(2,1)}), bf16[192,2,32,8,128]{4,3,2,1,0:T(8,128)(2,1)}, u32[]{:S(2)}, u32[]{:S(2)}) %all-to-all-start.4) | async-done | bytes 25165856 | tf_op jit(solution)/shard_map/all_to_all | solution.py:110
  858.6 36.9 %scatter_fusion.10 = bf16[144,32,8,128]{3,2,1,0:T(8,128)(2,1)} fusion(bf16[144,32,8,128]{3,2,1,0:T(8,128)(2,1)} %scatter_fusion, s32[192]{0:T(256)S(1)} %compare_select_fusion.16, bf16[192,32,8,128]{3,2,1,0:T(8,128)(2,1)} %get-tuple-element.119), kind=kCustom, calls=%fused_computation.35 | custom fusion | bytes 37749504 | tf_op jit(solution)/shard_map/scatter | solution.py:111
  946.0 30.4 %scatter_fusion.12 = bf16[144,32,8,128]{3,2,1,0:T(8,128)(2,1)} fusion(bf16[144,32,8,128]{3,2,1,0:T(8,128)(2,1)} %scatter_fusion.1, s32[192]{0:T(256)S(1)} %compare_select_fusion.16, bf16[192,32,8,128]{3,2,1,0:T(8,128)(2,1)} %get-tuple-element.120), kind=kCustom, calls=%fused_computation.37 | custom fusion | bytes 37749504 | tf_op jit(solution)/shard_map/scatter | solution.py:111
  1087.5 37.7 %fusion.210.clone.5 = bf16[24,14336]{1,0:T(8,128)(2,1)S(1)} fusion(bf16[24,4096]{1,0:T(8,128)(2,1)S(1)} %fusion.130, bf16[2,4096,14336]{2,1,0:T(8,128)(2,1)} %param.24), kind=kOutput, calls=%fused_computation.223.clone.clone.clone.2 | convolution fusion | flops 2821668864 | bytes 118325248 | tf_op jit(solution)/shard_map/dot_general | solution.py:93
  1125.2 37.6 %fusion.118 = bf16[24,4096]{1,0:T(8,128)(2,1)S(1)} fusion(bf16[2,14336,4096]{2,1,0:T(8,128)(2,1)} %param.25, bf16[24,4096]{1,0:T(8,128)(2,1)S(1)} %fusion.130, bf16[24,14336]{1,0:T(8,128)(2,1)S(1)} %fusion.210.clone.5), kind=kOutput, calls=%fused_computation.163 | convolution fusion | flops 2818867200 | bytes 118521856 | tf_op jit(solution)/shard_map/dot_general | solution.py:94
  1185.8 38.5 %fusion.196.clone.5 = bf16[24,14336]{1,0:T(8,128)(2,1)} fusion(bf16[24,4096]{1,0:T(8,128)(2,1)S(1)} %copy-done.59, bf16[2,4096,14336]{2,1,0:T(8,128)(2,1)} %param.24), kind=kOutput, calls=%fused_computation.215.clone.clone.clone.2 | convolution fusion | flops 2821668864 | bytes 118325248 | tf_op jit(solution)/shard_map/dot_general | solution.py:93
  1240.6 115.5 %all-to-all-done.7 = bf16[192,2,32,8,128]{4,3,2,1,0:T(8,128)(2,1)} async-done(((bf16[192,2,32,8,128]{4,3,2,1,0:T(8,128)(2,1)}), bf16[192,2,32,8,128]{4,3,2,1,0:T(8,128)(2,1)}, u32[]{:S(2)}, u32[]{:S(2)}) %all-to-all-start.7) | async-done | bytes 25165856 | tf_op jit(solution)/shard_map/all_to_all | solution.py:110
  1373.7 30.4 %scatter_fusion.17 = bf16[144,32,8,128]{3,2,1,0:T(8,128)(2,1)} fusion(bf16[144,32,8,128]{3,2,1,0:T(8,128)(2,1)} %scatter_fusion.5, s32[192]{0:T(256)S(1)} %copy-done.32, bf16[192,32,8,128]{3,2,1,0:T(8,128)(2,1)} %get-tuple-element.117), kind=kCustom, calls=%fused_computation.42 | custom fusion | bytes 37749504 | tf_op jit(solution)/shard_map/scatter | solution.py:111
  1432.0 31.2 %scatter_fusion.19 = bf16[144,32,8,128]{3,2,1,0:T(8,128)(2,1)} fusion(bf16[144,32,8,128]{3,2,1,0:T(8,128)(2,1)} %scatter_fusion.6, s32[192]{0:T(256)S(1)} %copy-done.32, bf16[192,32,8,128]{3,2,1,0:T(8,128)(2,1)} %get-tuple-element.118), kind=kCustom, calls=%fused_computation.44 | custom fusion | bytes 37749504 | tf_op jit(solution)/shard_map/scatter | solution.py:111
  1542.1 38.8 %fusion.148 = bf16[1,24,4096]{2,1,0:T(8,128)(2,1)} fusion(bf16[2,14336,4096]{2,1,0:T(8,128)(2,1)} %param.25, bf16[24,4096]{1,0:T(8,128)(2,1)S(1)} %copy-done.60, bf16[24,14336]{1,0:T(8,128)(2,1)} %fusion.196.clone.5), kind=kOutput, calls=%fused_computation.173 | convolution fusion | flops 2818867200 | bytes 118521856 | tf_op jit(solution)/shard_map/dot_general | solution.py:94
  1580.9 19.6 %pad_maximum_fusion.3 = bf16[144,2,32,8,128]{4,3,2,1,0:T(8,128)(2,1)} fusion(bf16[144,1,32,8,128]{4,3,2,1,0:T(8,128)(2,1)} %bitcast.387, bf16[144,1,32,8,128]{4,3,2,1,0:T(8,128)(2,1)} %bitcast.391), kind=kLoop, calls=%fused_computation.104 | loop fusion | flops 9437184 | bytes 37748736 | tf_op jit(solution)/shard_map/stack | solution.py:132
  1628.3 37.7 %fusion.224.clone.5 = bf16[24,14336]{1,0:T(8,128)(2,1)S(1)} fusion(bf16[24,4096]{1,0:T(8,128)(2,1)S(1)} %fusion.124, bf16[2,4096,14336]{2,1,0:T(8,128)(2,1)} %param.24), kind=kOutput, calls=%fused_computation.231.clone.clone.clone.2 | convolution fusion | flops 2821668864 | bytes 118325248 | tf_op jit(solution)/shard_map/dot_general | solution.py:93
  1666.0 37.6 %fusion.154 = bf16[1,24,4096]{2,1,0:T(8,128)(2,1)S(1)} fusion(bf16[2,14336,4096]{2,1,0:T(8,128)(2,1)} %param.25, bf16[24,4096]{1,0:T(8,128)(2,1)S(1)} %fusion.124, pred[24]{0:T(512)(128)(4,1)S(1)} %copy-done.56, bf16[24,14336]{1,0:T(8,128)(2,1)S(1)} %fusion.224.clone.5), kind=kOutput, calls=%fused_computation.175 | convolution fusion | flops 2818965504 | bytes 118521880 | tf_op jit(solution)/shard_map/dot_general | solution.py:94
  (458 shorter events, 779.8 us)
Async XLA Ops:
  7.2 70.9 %all-gather.5.cloned.1.call-start = ((), (), s32[]{:S(2)}) async-start(), calls=%async_computation.10 | async-start | bytes 2654208 | tf_op jit(solution)/shard_map/all_gather | solution.py:47
  38.6 130.9 %copy-start.29 = (s32[144]{0:T(256)}, s32[144]{0:T(256)S(1)}, u32[]{:S(2)}) copy-start(s32[144]{0:T(256)S(1)} %scatter_custom_fusion) | copy-start | bytes 1732
  46.6 74.5 %copy-start.42 = (s32[144]{0:T(256)}, s32[144]{0:T(256)S(1)}, u32[]{:S(2)}) copy-start(s32[144]{0:T(256)S(1)} %compare_select_fusion.17) | copy-start | bytes 1732
  135.2 51.7 %all-to-all-start.1 = ((f32[8,1,1536]{2,1,0:T(1,128)}), f32[8,1,1536]{2,1,0:T(1,128)S(1)}, u32[]{:S(2)}, u32[]{:S(2)}) async-start(f32[8,1,1536]{2,1,0:T(1,128)} %reshape.841), calls=%async_computation.1 | async-start | bytes 98304 | tf_op jit(solution)/shard_map/all_to_all | solution.py:64
  186.9 40.4 %all-to-all-start = ((f32[192,8,4,128]{3,1,2,0:T(8,128)}), f32[192,8,4,128]{3,1,2,0:T(8,128)S(1)}, u32[]{:S(2)}, u32[]{:S(2)}) async-start(f32[192,8,4,128]{3,1,2,0:T(8,128)} %scatter_fusion.3), calls=%async_computation | async-start | bytes 6291456 | tf_op jit(solution)/shard_map/all_to_all | solution.py:64
  189.4 173.8 %all-gather.7.cloned.1.call-start = ((), (), s32[]{:S(2)}) async-start(), calls=%async_computation.11 | async-start | bytes 2654208 | tf_op jit(solution)/shard_map/all_gather | solution.py:47
  421.0 49.9 %all-to-all-start.3 = ((f32[8,1,1536]{2,1,0:T(1,128)}), f32[8,1,1536]{2,1,0:T(1,128)S(1)}, u32[]{:S(2)}, u32[]{:S(2)}) async-start(f32[8,1,1536]{2,1,0:T(1,128)} %reshape.847), calls=%async_computation.3 | async-start | bytes 98304 | tf_op jit(solution)/shard_map/all_to_all | solution.py:64
  471.5 79.1 %all-to-all-start.2 = ((f32[192,8,4,128]{3,1,2,0:T(8,128)}), f32[192,8,4,128]{3,1,2,0:T(8,128)S(1)}, u32[]{:S(2)}, u32[]{:S(2)}) async-start(f32[192,8,4,128]{3,1,2,0:T(8,128)} %scatter_fusion.8), calls=%async_computation.2 | async-start | bytes 6291456 | tf_op jit(solution)/shard_map/all_to_all | solution.py:64
  552.3 288.7 %all-to-all-start.4 = ((bf16[192,2,32,8,128]{4,3,2,1,0:T(8,128)(2,1)}), bf16[192,2,32,8,128]{4,3,2,1,0:T(8,128)(2,1)}, u32[]{:S(2)}, u32[]{:S(2)}) async-start(bf16[192,2,32,8,128]{4,3,2,1,0:T(8,128)(2,1)} %pad_maximum_fusion), calls=%async_computation.4 | async-start | bytes 50331648 | tf_op jit(solution)/shard_map/all_to_all | solution.py:110
  557.4 155.9 %all-gather.9.cloned.1.call-start = ((), (), s32[]{:S(2)}) async-start(), calls=%async_computation.12 | async-start | bytes 2654208 | tf_op jit(solution)/shard_map/all_gather | solution.py:47
  584.2 418.1 %copy-start.27 = (s32[144]{0:T(256)}, s32[144]{0:T(256)S(1)}, u32[]{:S(2)}) copy-start(s32[144]{0:T(256)S(1)} %scatter_custom_fusion.12) | copy-start | bytes 1732
  590.9 343.0 %copy-start.33 = (s32[1024]{0:T(1024)}, s32[1024]{0:T(1024)S(1)}, u32[]{:S(2)}) copy-start(s32[1024]{0:T(1024)S(1)} %pad_clamp_fusion.3) | copy-start | bytes 12292
  593.9 352.2 %copy-start.31 = (s32[192]{0:T(256)}, s32[192]{0:T(256)S(1)}, u32[]{:S(2)}) copy-start(s32[192]{0:T(256)S(1)} %compare_select_fusion.16) | copy-start | bytes 2308
  593.9 382.6 %copy-start.5 = (s32[192,1]{0,1:T(1,128)}, s32[192,1]{0,1:T(1,128)S(1)}, u32[]{:S(2)}) copy-start(s32[192,1]{0,1:T(1,128)S(1)} %or_select_fusion) | copy-start | bytes 2308
  858.6 54.8 %copy-start.11 = (bf16[144,8,4,128]{3,2,1,0:T(4,128)(2,1)S(1)}, bf16[144,8,4,128]{3,2,1,0:T(4,128)(2,1)}, u32[]{:S(2)}) copy-start(bf16[144,8,4,128]{3,2,1,0:T(4,128)(2,1)} %reshape.388) | copy-start | bytes 3538948
  858.6 54.8 %copy-start.20 = (pred[144,32]{1,0:T(8,128)(4,1)S(1)}, pred[144,32]{1,0:T(8,128)(4,1)}, u32[]{:S(2)}) copy-start(pred[144,32]{1,0:T(8,128)(4,1)} %fusion.322) | copy-start | bytes 13828
  942.6 77.7 %all-to-all-start.6 = ((f32[8,1,1536]{2,1,0:T(1,128)}), f32[8,1,1536]{2,1,0:T(1,128)S(1)}, u32[]{:S(2)}, u32[]{:S(2)}) async-start(f32[8,1,1536]{2,1,0:T(1,128)} %reshape.843), calls=%async_computation.6 | async-start | bytes 98304 | tf_op jit(solution)/shard_map/all_to_all | solution.py:64
  1020.3 47.0 %all-to-all-start.5 = ((f32[192,8,4,128]{3,1,2,0:T(8,128)}), f32[192,8,4,128]{3,1,2,0:T(8,128)S(1)}, u32[]{:S(2)}, u32[]{:S(2)}) async-start(f32[192,8,4,128]{3,1,2,0:T(8,128)} %scatter_fusion.15), calls=%async_computation.5 | async-start | bytes 6291456 | tf_op jit(solution)/shard_map/all_to_all | solution.py:64
  1067.3 288.7 %all-to-all-start.7 = ((bf16[192,2,32,8,128]{4,3,2,1,0:T(8,128)(2,1)}), bf16[192,2,32,8,128]{4,3,2,1,0:T(8,128)(2,1)}, u32[]{:S(2)}, u32[]{:S(2)}) async-start(bf16[192,2,32,8,128]{4,3,2,1,0:T(8,128)(2,1)} %pad_maximum_fusion.1), calls=%async_computation.7 | async-start | bytes 50331648 | tf_op jit(solution)/shard_map/all_to_all | solution.py:110
  1072.6 163.3 %all-gather.11.cloned.1.call-start = ((), (), s32[]{:S(2)}) async-start(), calls=%async_computation.13 | async-start | bytes 2654208 | tf_op jit(solution)/shard_map/all_gather | solution.py:47
  1240.6 133.1 %copy-start.32 = (s32[192]{0:T(256)S(1)}, s32[192]{0:T(256)}, u32[]{:S(2)}) copy-start(s32[192]{0:T(256)} %copy-done.31) | copy-start | bytes 2308
  1373.6 48.5 %copy-start.12 = (bf16[144,8,4,128]{3,2,1,0:T(4,128)(2,1)S(1)}, bf16[144,8,4,128]{3,2,1,0:T(4,128)(2,1)}, u32[]{:S(2)}) copy-start(bf16[144,8,4,128]{3,2,1,0:T(4,128)(2,1)} %reshape.393) | copy-start | bytes 3538948
  1482.6 52.5 %all-to-all-start.9 = ((f32[8,1,1536]{2,1,0:T(1,128)}), f32[8,1,1536]{2,1,0:T(1,128)S(1)}, u32[]{:S(2)}, u32[]{:S(2)}) async-start(f32[8,1,1536]{2,1,0:T(1,128)} %reshape.845), calls=%async_computation.9 | async-start | bytes 98304 | tf_op jit(solution)/shard_map/all_to_all | solution.py:64
  1535.1 78.8 %all-to-all-start.8 = ((f32[192,8,4,128]{3,1,2,0:T(8,128)}), f32[192,8,4,128]{3,1,2,0:T(8,128)S(1)}, u32[]{:S(2)}, u32[]{:S(2)}) async-start(f32[192,8,4,128]{3,1,2,0:T(8,128)} %scatter_fusion.22), calls=%async_computation.8 | async-start | bytes 6291456 | tf_op jit(solution)/shard_map/all_to_all | solution.py:64
  (61 other events, 951.6 us)
Sparse Core Ops, SparseCore 0:
  32.2 25.8 all-gather.4
  340.2 23.0 all-gather.6
  580.5 132.8 all-gather.8
  1185.9 49.9 all-gather.10
where the time goes:
time: 1730 us; the launch traced here: 1710 us
  local copies, waits for them, and re-layouts  520 us (30%)
  matrix products  510 us (29%)
  waiting for transfers between devices  381 us (22%)
  other arithmetic  236 us (14%)
  starting transfers between devices  48.3 us (3%)
    all_to_all x2, waiting for transfers between devices, migrate(): incoming = lax.all_to_all(outgoing, 'kv', 0, 0, tiled=True)  184 us
    dot_general x4, matrix products, finish_block(): jnp.dot(mixed_rows, w_up[layer_idx], preferred_element_type=jnp.float32)  152 us
    dot_general x4, matrix products, finish_block(): jnp.dot(inner_act, w_down[layer_idx], preferred_element_type=jnp.float32)  152 us
    all_gather x4, waiting for transfers between devices, project_all(): gathered = lax.all_gather(packed, 'kv', axis=0, tiled=True)  146 us
    scatter x4, local copies, waits for them, and re-layouts, write_new(): k_layer.at[write_rows, offset].set(k_new, mode='drop')  80.1 us
    scatter x4, local copies, waits for them, and re-layouts, write_new(): v_layer.at[write_rows, offset].set(v_new, mode='drop')  78.1 us
    scatter-add x4, other arithmetic, attend(): jax.ops.segment_sum(slot_out * factor[..., None], slot_owner, num_segment...  70.7 us
    scatter x2, local copies, waits for them, and re-layouts, migrate(): k_layer.at[recv_slot].set(incoming[:, 0], mode='drop')  67.4 us
  transfers between devices with their start and end apart: 14, of which 7 were waited for; matrix products, arithmetic and copies ran while one was open for 40% of the time, Pallas kernels for 0%

commit v1 on v0

v1 whole, which is shorter than its diff:
```python
import functools

import jax
import jax.numpy as jnp
from jax import lax
from jax.experimental import pallas as pl
from jax.experimental.pallas import tpu as pltpu
from jax.sharding import PartitionSpec as P


MESH = pl.DeviceIdType.MESH
ANY = pl.BlockSpec(memory_space=pl.ANY)
VMEM = pl.BlockSpec(memory_space=pltpu.VMEM)
SMEM = pl.BlockSpec(memory_space=pltpu.SMEM)
NEG = -3e38
ENTRY_PAD = 160
GROUP = 4
DEPTH = 6
RING = 16
LAG = 8
CHUNKS = ((0, 0, 3), (0, 3, 13), (0, 13, 24), (1, 0, 16), (1, 16, 24))


def peers():
    rep = lax.axis_index('rep')
    me = lax.axis_index('kv')
    core = lax.rem(me, 2)
    chip = me // 2
    x = lax.rem(chip, 2)
    y = chip // 2
    partner = me + 1 - 2 * core
    chips = (y * 2 + (1 - x), (1 - y) * 2 + x, (1 - y) * 2 + (1 - x))
    return rep, me, core, chip, partner, chips


def meet(rep, others):
    barrier = pltpu.get_barrier_semaphore()
    for other in others:
        pl.semaphore_signal(barrier, inc=1, device_id=(rep, other), device_id_type=MESH)
    pl.semaphore_wait(barrier, len(others))


def gather_kernel(x_ref, out_ref, local_sem, send_sems, recv_sems):
    rep, me, core, _, partner, chips = peers()
    same = [c * 2 + core for c in chips]
    meet(rep, same + [partner])
    own = pltpu.make_async_copy(x_ref, out_ref.at[me], local_sem)

    def remote(src, dst_at, k, dev):
        return pltpu.make_async_remote_copy(src_ref=src, dst_ref=out_ref.at[dst_at], send_sem=send_sems.at[k], recv_sem=recv_sems.at[k], device_id=(rep, dev), device_id_type=MESH)

    across = [remote(x_ref, me, k, same[k]) for k in (2, 0, 1)]
    for copy in across:
        copy.start()
    to_partner = remote(x_ref, me, 3, partner)
    to_partner.start()
    own.start()
    forwards = []
    for k in (0, 1, 2):
        remote(x_ref, me, k, same[k]).wait_recv()
        forward = remote(out_ref.at[same[k]], same[k], 4 + k, partner)
        forward.start()
        forwards.append(forward)
    own.wait()
    for copy in across:
        copy.wait_send()
    to_partner.wait()
    for forward in forwards:
        forward.wait()


def gather_rows(x, collective_id, groups):
    return pl.pallas_call(
        gather_kernel,
        out_shape=jax.ShapeDtypeStruct((groups,) + x.shape, x.dtype),
        in_specs=[VMEM],
        out_specs=ANY,
        scratch_shapes=[pltpu.SemaphoreType.DMA, pltpu.SemaphoreType.DMA((7,)), pltpu.SemaphoreType.DMA((7,))],
        compiler_params=pltpu.CompilerParams(collective_id=collective_id, has_side_effects=True),
        name='gather_rows',
    )(x)


def swap_kernel(o_ref, s_ref, o_out, s_out, send_sems, recv_sems):
    rep, _, core, _, partner, _ = peers()
    meet(rep, [partner])
    copies = []
    for c in range(4):
        theirs = c * 2 + (1 - core)
        copies.append(pltpu.make_async_remote_copy(src_ref=o_ref.at[theirs], dst_ref=o_out.at[c], send_sem=send_sems.at[c], recv_sem=recv_sems.at[c], device_id=(rep, partner), device_id_type=MESH))
        copies.append(pltpu.make_async_remote_copy(src_ref=s_ref.at[theirs], dst_ref=s_out.at[c], send_sem=send_sems.at[4 + c], recv_sem=recv_sems.at[4 + c], device_id=(rep, partner), device_id_type=MESH))
    for copy in copies:
        copy.start()
    for copy in copies:
        copy.wait()


def swap_partials(o, s, collective_id):
    return pl.pallas_call(
        swap_kernel,
        out_shape=(jax.ShapeDtypeStruct((4,) + o.shape[1:], o.dtype), jax.ShapeDtypeStruct((4,) + s.shape[1:], s.dtype)),
        in_specs=[ANY, ANY],
        out_specs=(ANY, ANY),
        scratch_shapes=[pltpu.SemaphoreType.DMA((8,)), pltpu.SemaphoreType.DMA((8,))],
        compiler_params=pltpu.CompilerParams(collective_id=collective_id, has_side_effects=True),
        name='swap_partials',
    )(o, s)


def home_kernel(o_ref, s_ref, o_out, s_out, send_sems, recv_sems):
    rep, _, core, _, _, chips = peers()
    same = [c * 2 + core for c in chips]
    meet(rep, same)
    copies = []
    for k in (2, 0, 1):
        copies.append(pltpu.make_async_remote_copy(src_ref=o_ref.at[chips[k]], dst_ref=o_out.at[k], send_sem=send_sems.at[k], recv_sem=recv_sems.at[k], device_id=(rep, same[k]), device_id_type=MESH))
        copies.append(pltpu.make_async_remote_copy(src_ref=s_ref.at[chips[k]], dst_ref=s_out.at[k], send_sem=send_sems.at[3 + k], recv_sem=recv_sems.at[3 + k], device_id=(rep, same[k]), device_id_type=MESH))
    for copy in copies:
        copy.start()
    for copy in copies:
        copy.wait()


def home_partials(o, s, collective_id):
    return pl.pallas_call(
        home_kernel,
        out_shape=(jax.ShapeDtypeStruct((3,) + o.shape[1:], o.dtype), jax.ShapeDtypeStruct((3,) + s.shape[1:], s.dtype)),
        in_specs=[ANY, ANY],
        out_specs=(ANY, ANY),
        scratch_shapes=[pltpu.SemaphoreType.DMA((6,)), pltpu.SemaphoreType.DMA((6,))],
        compiler_params=pltpu.CompilerParams(collective_id=collective_id, has_side_effects=True),
        name='home_partials',
    )(o, s)


def attend_kernel(layer, n_seq, heads, scale, list_ref, q_ref, k_hbm, v_hbm, o_ref, m_out, l_out, m_acc, l_acc, kbuf, vbuf, sems):
    rows, dim = q_ref.shape[1:]
    keys = kbuf.shape[2]
    n_groups = (list_ref[3, 0] + GROUP - 1) // GROUP

    def copies(g, buf):
        out = []
        for j in range(GROUP):
            slot = list_ref[1, g * GROUP + j]
            out.append(pltpu.make_async_copy(k_hbm.at[slot, layer], kbuf.at[buf, j], sems.at[buf]))
            out.append(pltpu.make_async_copy(v_hbm.at[slot, layer], vbuf.at[buf, j], sems.at[buf]))
        return out

    for g in range(DEPTH):
        @pl.when(g < n_groups)
        def _():
            for copy in copies(g, g):
                copy.start()

    def clear(i, carry):
        o_ref[i] = jnp.zeros((rows, dim), jnp.float32)
        m_acc[i] = jnp.full((rows, dim), NEG, jnp.float32)
        l_acc[i] = jnp.zeros((rows, dim), jnp.float32)
        return carry

    lax.fori_loop(0, n_seq, clear, 0)

    row = lax.broadcasted_iota(jnp.int32, (rows, keys), 0)
    col = lax.broadcasted_iota(jnp.int32, (rows, keys), 1)
    same_head = lax.rem(col, heads) == lax.rem(row, rows // 2) // (rows // 2 // heads)
    position = jnp.where(same_head, col // heads, keys)

    def group(g, carry):
        buf = lax.rem(g, DEPTH)
        for copy in copies(g, buf):
            copy.wait()
        parts = []
        for j in range(GROUP):
            e = g * GROUP + j
            seq = list_ref[0, e]
            mask = position < list_ref[2, e]
            scores = lax.dot_general(q_ref[seq], kbuf[buf, j], (((1,), (1,)), ((), ())), preferred_element_type=jnp.float32) * scale
            scores = jnp.where(mask, scores, NEG)
            top = jnp.max(scores, axis=1, keepdims=True)
            weights = jnp.where(mask, jnp.exp(scores - top), 0.0)
            total = jnp.sum(weights, axis=1, keepdims=True)
            mixed = jnp.dot(weights.astype(jnp.bfloat16), vbuf[buf, j], preferred_element_type=jnp.float32)
            parts.append((seq, top, total, mixed))
        for seq, top, total, mixed in parts:
            top_old = m_acc[seq]
            top_new = jnp.maximum(top_old, top)
            keep = jnp.exp(top_old - top_new)
            add = jnp.exp(top - top_new)
            m_acc[seq] = top_new
            l_acc[seq] = l_acc[seq] * keep + total * add
            o_ref[seq] = o_ref[seq] * keep + mixed * add

        @pl.when(g + DEPTH < n_groups)
        def _():
            for copy in copies(g + DEPTH, buf):
                copy.start()

        return carry

    lax.fori_loop(0, n_groups, group, 0)

    lane = lax.broadcasted_iota(jnp.int32, (rows, dim), 1)
    for part in range(2):
        first = part * dim
        many = min(dim, n_seq - first)

        def pack(i, carry):
            tops, totals = carry
            here = lane == i
            return jnp.where(here, m_acc[first + i], tops), jnp.where(here, l_acc[first + i], totals)

        zero = jnp.zeros((rows, dim), jnp.float32)
        tops, totals = lax.fori_loop(0, many, pack, (zero, zero))
        m_out[:, first:first + dim] = tops
        l_out[:, first:first + dim] = totals


def attend_pages(lists, q_all, k_pool, v_pool, layer, heads, scale):
    n_seq, rows, dim = q_all.shape
    keys = k_pool.shape[2]
    return pl.pallas_call(
        functools.partial(attend_kernel, layer, n_seq, heads, scale),
        out_shape=(
            jax.ShapeDtypeStruct((n_seq, rows, dim), jnp.float32),
            jax.ShapeDtypeStruct((rows, 2 * dim), jnp.float32),
            jax.ShapeDtypeStruct((rows, 2 * dim), jnp.float32),
        ),
        in_specs=[SMEM, VMEM, ANY, ANY],
        out_specs=(VMEM, VMEM, VMEM),
        scratch_shapes=[
            pltpu.VMEM((n_seq, rows, dim), jnp.float32),
            pltpu.VMEM((n_seq, rows, dim), jnp.float32),
            pltpu.VMEM((DEPTH, GROUP, keys, dim), k_pool.dtype),
            pltpu.VMEM((DEPTH, GROUP, keys, dim), v_pool.dtype),
            pltpu.SemaphoreType.DMA((DEPTH,)),
        ],
        compiler_params=pltpu.CompilerParams(vmem_limit_bytes=48 * 1024 * 1024),
        cost_estimate=pl.CostEstimate(flops=40_000_000_000, bytes_accessed=30_000_000, transcendentals=0),
        name='attend_pages',
    )(lists, q_all, k_pool, v_pool)


def patch_kernel(list_ref, rows_ref, k_in, v_in, k_out, v_out, sem):
    many = list_ref[3, 0]

    def copies(i):
        row, slot, offset = list_ref[0, i], list_ref[1, i], list_ref[2, i]
        return [pltpu.make_async_copy(rows_ref.at[row, kind], ref.at[slot, :, offset], sem) for kind, ref in ((0, k_out), (1, v_out))]

    def start(i, carry):
        for copy in copies(i):
            copy.start()
        return carry

    def finish(i, carry):
        for copy in copies(i):
            copy.wait()
        return carry

    lax.fori_loop(0, many, start, 0)
    lax.fori_loop(0, many, finish, 0)


def patch_pools(writes, rows, k_pool, v_pool):
    return pl.pallas_call(
        patch_kernel,
        out_shape=(jax.ShapeDtypeStruct(k_pool.shape, k_pool.dtype), jax.ShapeDtypeStruct(v_pool.shape, v_pool.dtype)),
        in_specs=[SMEM, VMEM, ANY, ANY],
        out_specs=(ANY, ANY),
        scratch_shapes=[pltpu.SemaphoreType.DMA],
        input_output_aliases={2: 0, 3: 1},
        name='patch_pools',
    )(writes, rows, k_pool, v_pool)


def move_kernel(list_ref, src_ref, *refs):
    dst_ref, ring, in_sems, out_sems = refs[-4:]
    many = list_ref[2, 0]

    def fetch(i):
        buf = lax.rem(i, RING)
        return pltpu.make_async_copy(src_ref.at[list_ref[0, i]], ring.at[buf], in_sems.at[buf])

    def store(i):
        buf = lax.rem(i, RING)
        return pltpu.make_async_copy(ring.at[buf], dst_ref.at[list_ref[1, i]], out_sems.at[buf])

    def first(i, carry):
        fetch(i).start()
        return carry

    def step(i, carry):
        fetch(i).wait()
        store(i).start()

        @pl.when(i >= LAG)
        def _():
            store(i - LAG).wait()

            @pl.when(i - LAG + RING < many)
            def _():
                fetch(i - LAG + RING).start()

        return carry

    def last(i, carry):
        store(i).wait()
        return carry

    lax.fori_loop(0, jnp.minimum(many, RING), first, 0)
    lax.fori_loop(0, many, step, 0)
    lax.fori_loop(jnp.maximum(many - LAG, 0), many, last, 0)


def move_pages(moves, src, dst):
    fresh = isinstance(dst, tuple)
    shape = dst if fresh else dst.shape
    return pl.pallas_call(
        move_kernel,
        out_shape=jax.ShapeDtypeStruct(shape, src.dtype),
        in_specs=[SMEM, ANY] if fresh else [SMEM, ANY, ANY],
        out_specs=ANY,
        scratch_shapes=[pltpu.VMEM((RING,) + src.shape[1:], src.dtype), pltpu.SemaphoreType.DMA((RING,)), pltpu.SemaphoreType.DMA((RING,))],
        input_output_aliases={} if fresh else {2: 0},
    )(*((moves, src) if fresh else (moves, src, dst)))


def compact(keep, size, *columns):
    n = keep.shape[-1]
    place = jnp.arange(n, dtype=jnp.int32)
    before = (place[:, None] < place[None, :]).astype(jnp.bfloat16)
    rank = jnp.dot(keep.astype(jnp.bfloat16), before, preferred_element_type=jnp.float32).astype(jnp.int32)
    rank = jnp.where(keep, rank, -1)
    hit = rank[:, None, :] == jnp.arange(size, dtype=jnp.int32)[None, :, None]
    packed = [jnp.sum(jnp.where(hit, column[:, None, :], 0), axis=-1) for column in columns]
    many = jnp.sum(keep.astype(jnp.int32), axis=-1)
    return jnp.stack(packed + [jnp.broadcast_to(many[:, None], packed[0].shape)], axis=1)


def solution(mesh):
    groups = mesh.shape['kv']
    rows_spec = P(None, ('rep', 'kv'), None)
    pool_spec = P(('rep', 'kv'))
    table_spec = P('rep', None)
    vec_spec = P('rep')
    full_spec = P()

    def device_fn(embeds, w_query, w_key, w_value, w_out, w_up, w_down, k_pool, v_pool, old_table, new_table, seq_len, finished, mig_src, mig_dst):
        my_dev = lax.axis_index('kv')
        slots_dev, n_layers, page_size, kv_heads, head_dim = k_pool.shape
        n_steps, seq_dev, d_model = embeds.shape
        n_batch, pages_seq = old_table.shape
        q_width = w_query.shape[2]
        kv_width = kv_heads * head_dim
        rep_factor = q_width // kv_width
        q_heads = kv_heads * rep_factor
        n_mig = mig_src.shape[0]
        scale = head_dim ** -0.5
        slot_base = my_dev * slots_dev
        last_page = pages_seq - 1
        active = finished == 0

        src_dev = mig_src // slots_dev
        dst_dev = mig_dst // slots_dev
        pair_key = src_dev * groups + dst_dev
        entry_ids = jnp.arange(n_mig, dtype=jnp.int32)
        earlier = (pair_key[None, :] == pair_key[:, None]) & (entry_ids[None, :] < entry_ids[:, None])
        pair_rank = jnp.sum(earlier.astype(jnp.int32), axis=1)
        keeps, froms, tos = [], [], []
        for pool, low, high in CHUNKS:
            wide = high - low
            ranked = (pair_rank >= low) & (pair_rank < high)
            keeps.append(ranked & (src_dev == my_dev))
            froms.append(mig_src - slot_base)
            tos.append(dst_dev * wide + pair_rank - low)
            keeps.append(ranked & (dst_dev == my_dev))
            froms.append(src_dev * wide + pair_rank - low)
            tos.append(mig_dst - slot_base)
        plan = compact(jnp.stack(keeps), slots_dev, jnp.stack(froms), jnp.stack(tos))
        pools = (k_pool, v_pool)
        received = [None] * len(CHUNKS)

        def pack(c, after=None):
            pool, low, high = CHUNKS[c]
            moves = plan[2 * c]
            if after is not None:
                moves, _ = lax.optimization_barrier((moves, after))
            return move_pages(moves, pools[pool], (groups * (high - low),) + k_pool.shape[1:])

        def send(c, pages, after=None):
            if after is not None:
                pages, _ = lax.optimization_barrier((pages, after))
            received[c] = lax.all_to_all(pages, 'kv', 0, 0, tiled=True)

        page_slot = old_table.reshape(-1) - slot_base
        here = (page_slot >= 0) & (page_slot < slots_dev)
        page_seq = jnp.repeat(jnp.arange(n_batch, dtype=jnp.int32), pages_seq)
        page_start = jnp.tile(jnp.arange(pages_seq, dtype=jnp.int32) * page_size, n_batch)
        page_valid = jnp.clip(jnp.repeat(seq_len, pages_seq) - page_start, 0, page_size)
        lists = compact(here[None], ENTRY_PAD, page_seq[None], page_slot[None], page_valid[None])[0]

        old_last = old_table[:, last_page]
        new_last = new_table[:, last_page]
        overwritten = jnp.any(old_last[:, None] == mig_dst[None, :], axis=1)
        moved = active & (new_last != old_last)
        seq_ids = jnp.arange(n_batch, dtype=jnp.int32)
        offset = seq_len - last_page * page_size
        write_slot = jnp.concatenate([jnp.where(overwritten, -1, old_last), jnp.where(moved, new_last, -1), jnp.where(active, new_last, -1)]) - slot_base
        write_row = jnp.concatenate([seq_ids * 2, seq_ids * 2, seq_ids * 2 + 1])
        write_offset = jnp.concatenate([offset, offset, offset + 1])
        write_here = (write_slot >= 0) & (write_slot < slots_dev)
        writes = compact(write_here[None], 2 * slots_dev, write_row[None], write_slot[None], write_offset[None])[0]

        k_pages = k_pool.reshape(slots_dev, n_layers, page_size * kv_heads, head_dim)
        v_pages = v_pool.reshape(slots_dev, n_layers, page_size * kv_heads, head_dim)
        rows = seq_dev * n_steps
        lanes = n_steps * q_heads

        def dot(a, b):
            return jnp.dot(a, b, preferred_element_type=jnp.float32)

        def split(stats):
            return stats[..., :lanes], stats[..., lanes:]

        send(0, pack(0))
        hidden = embeds.transpose(1, 0, 2).reshape(rows, d_model)
        new_rows = []
        for layer in range(n_layers):
            query = dot(hidden, w_query[layer]).astype(jnp.bfloat16).reshape(seq_dev, lanes, head_dim)
            k_new = dot(hidden, w_key[layer]).astype(jnp.bfloat16).reshape(seq_dev, n_steps, kv_heads, head_dim)
            v_new = dot(hidden, w_value[layer]).astype(jnp.bfloat16).reshape(seq_dev, n_steps, kv_heads, head_dim)
            new_rows.append(jnp.stack([k_new, v_new], axis=2))

            packed = pack(layer + 1, query)
            q_all = gather_rows(query, 3 * layer, groups).reshape(n_batch, lanes, head_dim)
            o_part, m_part, l_part = attend_pages(lists, q_all, k_pages, v_pages, layer, kv_heads, scale)
            stats = jnp.concatenate([m_part.T[:n_batch], l_part.T[:n_batch]], axis=1).reshape(groups, seq_dev, 2 * lanes)
            o_part = o_part.reshape(groups, seq_dev, lanes, head_dim)

            o_recv, s_recv = swap_partials(o_part, stats, 3 * layer + 1)
            core = lax.rem(my_dev, 2)
            chip = my_dev // 2
            o_mine = lax.dynamic_index_in_dim(o_part.reshape(groups // 2, 2, seq_dev, lanes, head_dim), core, 1, keepdims=False)
            s_mine = lax.dynamic_index_in_dim(stats.reshape(groups // 2, 2, seq_dev, 2 * lanes), core, 1, keepdims=False)
            m_a, l_a = split(s_mine)
            m_b, l_b = split(s_recv)
            m_chip = jnp.maximum(m_a, m_b)
            f_a, f_b = jnp.exp(m_a - m_chip), jnp.exp(m_b - m_chip)
            o_chip = o_mine * f_a[..., None] + o_recv * f_b[..., None]
            s_chip = jnp.concatenate([m_chip, l_a * f_a + l_b * f_b], axis=-1)

            o_far, s_far = home_partials(o_chip, s_chip, 3 * layer + 2)
            send(layer + 1, packed, o_far)
            o_near = lax.dynamic_index_in_dim(o_chip, chip, 0, keepdims=False)
            m_near, l_near = split(lax.dynamic_index_in_dim(s_chip, chip, 0, keepdims=False))
            m_far, l_far = split(s_far)
            q_own = query.astype(jnp.float32).reshape(seq_dev, n_steps, 1, kv_heads, rep_factor, head_dim)
            k_own = k_new.astype(jnp.float32).reshape(seq_dev, 1, n_steps, kv_heads, 1, head_dim)
            own = jnp.sum(q_own * k_own, axis=-1) * scale
            seen = jnp.arange(n_steps)[None, :] <= jnp.arange(n_steps)[:, None]
            own = jnp.where(seen[None, :, :, None, None], own, NEG)
            m_own = own.max(axis=2).reshape(seq_dev, lanes)
            m_all = jnp.maximum(jnp.maximum(m_near, m_far.max(axis=0)), m_own)
            p_own = jnp.exp(own - m_all.reshape(seq_dev, n_steps, 1, kv_heads, rep_factor))
            v_own = v_new.astype(jnp.float32).reshape(seq_dev, 1, n_steps, kv_heads, 1, head_dim)
            o_own = jnp.sum(p_own[..., None] * v_own, axis=2).reshape(seq_dev, lanes, head_dim)
            f_near = jnp.exp(m_near - m_all)
            f_far = jnp.exp(m_far - m_all)
            total = l_near * f_near + jnp.sum(l_far * f_far, axis=0) + jnp.sum(p_own, axis=2).reshape(seq_dev, lanes)
            o_all = o_own + o_near * f_near[..., None]
            for k in range(3):
                o_all = o_all + o_far[k] * f_far[k][..., None]
            attn = (o_all / total[..., None]).astype(jnp.bfloat16).reshape(rows, q_width)

            mixed = (hidden.astype(jnp.float32) + dot(attn, w_out[layer])).astype(jnp.bfloat16)
            inner = jax.nn.gelu(dot(mixed, w_up[layer])).astype(jnp.bfloat16)
            hidden = (mixed.astype(jnp.float32) + dot(inner, w_down[layer])).astype(jnp.bfloat16)

        rows_here = jnp.stack(new_rows, axis=3)
        rows_all = lax.all_gather(rows_here, 'kv', axis=0, tiled=True).reshape(n_batch * n_steps, 2, n_layers, kv_heads, head_dim)

        for c in range(n_layers + 1, len(CHUNKS)):
            send(c, pack(c, hidden))
        slot_ids = jnp.arange(slots_dev, dtype=jnp.int32)
        every = jnp.stack([slot_ids, slot_ids, jnp.full((slots_dev,), slots_dev, jnp.int32)])
        every, takes, _ = lax.optimization_barrier((every, plan[1::2], hidden))
        outs = [move_pages(every, pool, pool.shape) for pool in pools]
        for c, (pool, low, high) in enumerate(CHUNKS):
            outs[pool] = move_pages(takes[c], received[c], outs[pool])
        k_out, v_out = patch_pools(writes, rows_all, *outs)

        home_done = lax.dynamic_slice(finished, (my_dev * seq_dev,), (seq_dev,))
        hidden = hidden.reshape(seq_dev, n_steps, d_model)
        hid_one = jnp.where(home_done[:, None] == 0, hidden[:, 1], jnp.zeros_like(hidden[:, 1]))
        return jnp.stack([hidden[:, 0], hid_one]), k_out, v_out

    in_specs = (rows_spec, full_spec, full_spec, full_spec, full_spec, full_spec, full_spec, pool_spec, pool_spec, table_spec, table_spec, vec_spec, vec_spec, vec_spec, vec_spec)

    return jax.shard_map(device_fn, mesh=mesh, in_specs=in_specs, out_specs=(rows_spec, pool_spec, pool_spec), check_vma=False)
```

time: 1730 us -> 974 us (0.56)
  local copies, waits for them, and re-layouts: 520 us -> 20.6 us
  Pallas kernels: 0 us -> 371 us
  matrix products: 510 us -> 230 us
  other arithmetic: 236 us -> 33.9 us
  waiting for transfers between devices: 381 us -> 270 us
  starting transfers between devices: 48.3 us -> 20.9 us
    pallas_call x0 -> x21, Pallas kernels: none -> 371 us  [the longest x2 121 us: home_partials(): pl.pallas_call(home_kernel, out_shape=(jax.ShapeDtypeStruct((3,) + o.shap...]
    scatter x19 -> x0, local copies, waits for them, and re-layouts: 310 us -> none  [the longest x4 80.1 us: write_new(): k_layer.at[write_rows, offset].set(k_new, mode='drop')]
    dot_general x32 -> x15, matrix products: 510 us -> 230 us  [the longest x12 229 us: dot(): return jnp.dot(a, b, preferred_element_type=jnp.float32)]
    all_gather x4 -> x1, waiting for transfers between devices: 146 us -> 0.02 us  [device_fn(): lax.all_gather(rows_here, 'kv', axis=0, tiled=True)]
    scatter-add x8 -> x0, other arithmetic: 93.2 us -> none  [the longest x4 70.7 us: attend(): jax.ops.segment_sum(slot_out * factor[..., None], slot_owner, num_segment...]
    gather x30 -> x0, local copies, waits for them, and re-layouts: 91.5 us -> none  [the longest x4 47.3 us: migrate(): outgoing = jnp.stack([k_layer[send_slot], v_layer[send_slot]], axis=1)]
    another operation x9 -> x6, other arithmetic: 92 us -> 2.38 us  [the longest x3 0.9 us: device_fn(): rows_here = jnp.stack(new_rows, axis=3)]
    squeeze x4, local copies, waits for them, and re-layouts: 65.3 us -> 1.26 us  [the longest x1 0.62 us: device_fn(): outs[pool] = move_pages(takes[c], received[c], outs[pool])]
  transfers between devices with their start and end apart: 14 -> 6, of which waited for: 7 -> 3; matrix products, arithmetic and copies ran while one was open for 40% -> 29% of each run, Pallas kernels for 0% -> 38%
where the time goes in v1:
time: 974 us; the launch traced here: 961 us
  Pallas kernels  371 us (38%)
  waiting for transfers between devices  270 us (28%)
  matrix products  230 us (24%)
  other arithmetic  33.9 us (3%)
  starting transfers between devices  20.9 us (2%)
  local copies, waits for them, and re-layouts  20.6 us (2%)
  between operations  15.6 us (2%)
    all_to_all x5, waiting for transfers between devices, send(): received[c] = lax.all_to_all(pages, 'kv', 0, 0, tiled=True)  270 us
    dot_general x12, matrix products, dot(): return jnp.dot(a, b, preferred_element_type=jnp.float32)  229 us
    pallas_call x2, Pallas kernels, home_partials(): pl.pallas_call(home_kernel, out_shape=(jax.ShapeDtypeStruct((3,) + o.shap...  121 us
    pallas_call x2, Pallas kernels, attend_pages(): pl.pallas_call(functools.partial(attend_kernel, layer, n_seq, heads, scal...  91.1 us
    pallas_call x12, Pallas kernels, move_pages(): pl.pallas_call(move_kernel, out_shape=jax.ShapeDtypeStruct(shape, src.dty...  80.9 us
    pallas_call x2, Pallas kernels, gather_rows(): pl.pallas_call(gather_kernel, out_shape=jax.ShapeDtypeStruct((groups,) +...  62.2 us
    all_to_all x5, starting transfers between devices, send(): received[c] = lax.all_to_all(pages, 'kv', 0, 0, tiled=True)  20.9 us
  transfers between devices with their start and end apart: 6, of which 3 were waited for; matrix products, arithmetic and copies ran while one was open for 29% of the time, Pallas kernels for 38%

profile of v1, /device:TPU:0, one launch (start us, length us, event | category | flops | bytes accessed | tf_op | source)
XLA Modules:
  0.0 961.4 jit_solution(851247376505517485)
XLA Ops:
  19.4 13.6 %fusion.60 = bf16[48,4096]{1,0:T(8,128)(2,1)S(1)} fusion(bf16[48,4096]{1,0:T(8,128)(2,1)S(1)} %reshape.808, bf16[2,4096,4096]{2,1,0:T(8,128)(2,1)} %param.16), kind=kOutput, calls=%fused_computation.44 | convolution fusion | flops 1610809344 | bytes 34340864 | tf_op jit(solution)/shard_map/dot_general | solution.py:420
  36.9 38.8 %gather_rows.2 = bf16[8,24,64,128]{3,2,1,0:T(8,128)(2,1)} custom-call(bf16[24,64,128]{2,1,0:T(8,128)(2,1)} %reshape.809.x_ref), custom_call_target="tpu_custom_call" | custom-call | tf_op jit(solution)/shard_map/gather_rows/pallas_call | solution.py:73
  77.9 45.6 %attend_pages.2 = (f32[192,64,128]{2,1,0:T(8,128)}, f32[64,256]{1,0:T(8,128)S(1)}, f32[64,256]{1,0:T(8,128)S(1)}) custom-call(s32[4,160]{1,0:T(4,128)S(1)} %add_bitcast_fusion.1.list_ref, bf16[192,64,128]{2,1,0:T(8,128)(2,1)S(1)} %bitcast.313, bf16[144,2,256,128]{3,2,1,0:T(8,128)(2,1)} %bitcast.319, bf16[144,2,256,128]{3,2,1,0:T(8,128)(2,1)} %bitcast.321), custom_call_target="tpu_custom_call" | custom-call | flops 40000000000 | bytes 30000000 | tf_op jit(solution)/shard_map/attend_pages/pallas_call | solution.py:221
  124.3 6.2 swap_partials.2
  138.4 38.6 %home_partials.2 = (f32[3,24,64,128]{3,2,1,0:T(8,128)}, f32[3,24,128]{2,1,0:T(8,128)}) custom-call(f32[4,24,64,128]{3,2,1,0:T(8,128)} %fusion.67.o_ref, f32[4,24,128]{2,1,0:T(8,128)} %pad_maximum_fusion.4.s_ref), custom_call_target="tpu_custom_call" | custom-call | tf_op jit(solution)/shard_map/home_partials/pallas_call | solution.py:125
  194.7 13.7 %fusion.57 = bf16[48,4096]{1,0:T(8,128)(2,1)S(1)} fusion(bf16[48,4096]{1,0:T(8,128)(2,1)S(1)} %convert_element_type.187, bf16[2,4096,4096]{2,1,0:T(8,128)(2,1)} %param.19, bf16[48,4096]{1,0:T(8,128)(2,1)S(1)} %reshape.808), kind=kOutput, calls=%fused_computation.43 | convolution fusion | flops 1611202560 | bytes 34734080 | tf_op jit(solution)/shard_map/dot_general | solution.py:420
  208.4 38.8 %fusion.77.clone.5 = bf16[48,14336]{1,0:T(8,128)(2,1)S(1)} fusion(bf16[48,4096]{1,0:T(8,128)(2,1)S(1)} %fusion.57, bf16[2,4096,14336]{2,1,0:T(8,128)(2,1)} %param.20), kind=kOutput, calls=%fused_computation.59.clone.clone.clone.2 | convolution fusion | flops 5643337728 | bytes 119209984 | tf_op jit(solution)/shard_map/dot_general | solution.py:420
  247.1 38.9 %fusion.51 = bf16[48,4096]{1,0:T(8,128)(2,1)S(1)} fusion(bf16[2,14336,4096]{2,1,0:T(8,128)(2,1)} %param.21, bf16[48,4096]{1,0:T(8,128)(2,1)S(1)} %fusion.57, bf16[48,14336]{1,0:T(8,128)(2,1)S(1)} %fusion.77.clone.5), kind=kOutput, calls=%fused_computation.41 | convolution fusion | flops 5637734400 | bytes 119603200 | tf_op jit(solution)/shard_map/dot_general | solution.py:420
  286.0 13.6 %fusion.63 = bf16[48,4096]{1,0:T(8,128)(2,1)S(1)} fusion(bf16[48,4096]{1,0:T(8,128)(2,1)S(1)} %fusion.51, bf16[2,4096,4096]{2,1,0:T(8,128)(2,1)} %param.16), kind=kOutput, calls=%fused_computation.45 | convolution fusion | flops 1610809344 | bytes 34340864 | tf_op jit(solution)/shard_map/dot_general | solution.py:420
  302.1 23.5 %gather_rows.3 = bf16[8,24,64,128]{3,2,1,0:T(8,128)(2,1)} custom-call(bf16[24,64,128]{2,1,0:T(8,128)(2,1)} %reshape.818.x_ref), custom_call_target="tpu_custom_call" | custom-call | tf_op jit(solution)/shard_map/gather_rows/pallas_call | solution.py:73
  325.6 7.1 shard_map.167
  336.9 45.5 %attend_pages.3 = (f32[192,64,128]{2,1,0:T(8,128)}, f32[64,256]{1,0:T(8,128)S(1)}, f32[64,256]{1,0:T(8,128)S(1)}) custom-call(s32[4,160]{1,0:T(4,128)S(1)} %add_bitcast_fusion.1.list_ref, bf16[192,64,128]{2,1,0:T(8,128)(2,1)S(1)} %bitcast.314, bf16[144,2,256,128]{3,2,1,0:T(8,128)(2,1)} %bitcast.320, bf16[144,2,256,128]{3,2,1,0:T(8,128)(2,1)} %bitcast.322), custom_call_target="tpu_custom_call" | custom-call | flops 40000000000 | bytes 30000000 | tf_op jit(solution)/shard_map/attend_pages/pallas_call | solution.py:221
  390.4 6.2 swap_partials.3
  404.5 82.4 %home_partials.3 = (f32[3,24,64,128]{3,2,1,0:T(8,128)}, f32[3,24,128]{2,1,0:T(8,128)}) custom-call(f32[4,24,64,128]{3,2,1,0:T(8,128)} %fusion.66.o_ref, f32[4,24,128]{2,1,0:T(8,128)} %pad_maximum_fusion.5.s_ref), custom_call_target="tpu_custom_call" | custom-call | tf_op jit(solution)/shard_map/home_partials/pallas_call | solution.py:125
  498.0 7.7 shard_map.166
  505.7 13.7 %fusion.54 = bf16[48,4096]{1,0:T(8,128)(2,1)S(1)} fusion(bf16[48,4096]{1,0:T(8,128)(2,1)S(1)} %convert_element_type.203, bf16[2,4096,4096]{2,1,0:T(8,128)(2,1)} %param.19, bf16[48,4096]{1,0:T(8,128)(2,1)S(1)} %fusion.51), kind=kOutput, calls=%fused_computation.42 | convolution fusion | flops 1611202560 | bytes 34734080 | tf_op jit(solution)/shard_map/dot_general | solution.py:420
  523.6 38.8 %fusion.91.clone.5 = bf16[48,14336]{1,0:T(8,128)(2,1)S(1)} fusion(bf16[48,4096]{1,0:T(8,128)(2,1)S(1)} %fusion.54, bf16[2,4096,14336]{2,1,0:T(8,128)(2,1)} %param.20), kind=kOutput, calls=%fused_computation.67.clone.clone.clone.2 | convolution fusion | flops 5643337728 | bytes 119209984 | tf_op jit(solution)/shard_map/dot_general | solution.py:420
  562.4 38.3 %fusion.48 = bf16[48,4096]{1,0:T(8,128)(2,1)S(1)} fusion(bf16[2,14336,4096]{2,1,0:T(8,128)(2,1)} %param.21, bf16[48,4096]{1,0:T(8,128)(2,1)S(1)} %fusion.54, bf16[48,14336]{1,0:T(8,128)(2,1)S(1)} %fusion.91.clone.5), kind=kOutput, calls=%fused_computation.40 | convolution fusion | flops 5637734400 | bytes 119603200 | tf_op jit(solution)/shard_map/dot_general | solution.py:420
  600.8 10.2 %shard_map.174 = bf16[128,2,32,8,128]{4,3,2,1,0:T(8,128)(2,1)} custom-call(s32[3,144]{1,0:T(4,128)} %get-tuple-element.48.list_ref, bf16[144,2,32,8,128]{4,3,2,1,0:T(8,128)(2,1)} %src_ref.13), custom_call_target="tpu_custom_call" | custom-call | tf_op jit(solution)/shard_map/pallas_call | solution.py:318
  611.0 40.4 %all-to-all-done.src_ref = bf16[88,2,32,8,128]{4,3,2,1,0:T(8,128)(2,1)} async-done(((bf16[88,2,32,8,128]{4,3,2,1,0:T(8,128)(2,1)}), bf16[88,2,32,8,128]{4,3,2,1,0:T(8,128)(2,1)}, u32[]{:S(2)}, u32[]{:S(2)}) %all-to-all-start) | async-done | bytes 11534368 | tf_op jit(solution)/shard_map/all_to_all | solution.py:393
  662.0 177.8 %all-to-all-done.4.src_ref = bf16[128,2,32,8,128]{4,3,2,1,0:T(8,128)(2,1)} async-done(((bf16[128,2,32,8,128]{4,3,2,1,0:T(8,128)(2,1)}), bf16[128,2,32,8,128]{4,3,2,1,0:T(8,128)(2,1)}, u32[]{:S(2)}, u32[]{:S(2)}) %all-to-all-start.4) | async-done | bytes 16777248 | tf_op jit(solution)/shard_map/all_to_all | solution.py:393
  845.4 20.6 %shard_map.175.refs_0_ = bf16[144,2,32,8,128]{4,3,2,1,0:T(8,128)(2,1)} custom-call(s32[3,144]{1,0:T(4,128)} %add_add_fusion.list_ref, bf16[144,2,32,8,128]{4,3,2,1,0:T(8,128)(2,1)} %src_ref.13), custom_call_target="tpu_custom_call" | custom-call | tf_op jit(solution)/shard_map/pallas_call | solution.py:318
  866.1 20.7 %shard_map.169.refs_0_ = bf16[144,2,32,8,128]{4,3,2,1,0:T(8,128)(2,1)} custom-call(s32[3,144]{1,0:T(4,128)} %add_add_fusion.list_ref, bf16[144,2,32,8,128]{4,3,2,1,0:T(8,128)(2,1)} %src_ref.10), custom_call_target="tpu_custom_call" | custom-call | tf_op jit(solution)/shard_map/pallas_call | solution.py:318
  898.7 51.6 %all-to-all-done.3.src_ref = bf16[64,2,32,8,128]{4,3,2,1,0:T(8,128)(2,1)} async-done(((bf16[64,2,32,8,128]{4,3,2,1,0:T(8,128)(2,1)}), bf16[64,2,32,8,128]{4,3,2,1,0:T(8,128)(2,1)}, u32[]{:S(2)}, u32[]{:S(2)}) %all-to-all-start.3) | async-done | bytes 8388640 | tf_op jit(solution)/shard_map/all_to_all | solution.py:393
  (232 shorter events, 113.5 us)
Async XLA Ops:
  14.5 4.3 copy-start.6
  14.5 318.2 %all-to-all-start.2 = ((bf16[24,2,32,8,128]{4,3,2,1,0:T(8,128)(2,1)}), bf16[24,2,32,8,128]{4,3,2,1,0:T(8,128)(2,1)}, u32[]{:S(2)}, u32[]{:S(2)}) async-start(bf16[24,2,32,8,128]{4,3,2,1,0:T(8,128)(2,1)} %shard_map.168), calls=%async_computation.2 | async-start | bytes 6291456 | tf_op jit(solution)/shard_map/all_to_all | solution.py:393
  19.4 15.3 %copy-start.22 = (s32[192,4]{0,1:T(4,128)S(1)}, s32[192,4]{0,1:T(4,128)}, u32[]{:S(2)}) copy-start(s32[192,4]{0,1:T(4,128)} %param.24) | copy-start | bytes 9220
  19.4 15.3 %copy-start.23 = (s32[192]{0:T(256)S(1)}, s32[192]{0:T(256)}, u32[]{:S(2)}) copy-start(s32[192]{0:T(256)} %param.26) | copy-start | bytes 2308
  34.7 150.0 %copy-start.20 = (pred[2,2]{1,0:T(4,128)(4,1)}, pred[2,2]{1,0:T(4,128)(4,1)S(1)}, u32[]{:S(2)}) copy-start(pred[2,2]{1,0:T(4,128)(4,1)S(1)} %iota_compare_fusion.14) | copy-start | bytes 16
  76.0 1.9 copy-start
  124.3 6.2 copy-start.4
  177.8 6.6 copy-start.16
  332.7 4.2 copy-start.1
  332.7 186.7 %all-to-all-start.1 = ((bf16[80,2,32,8,128]{4,3,2,1,0:T(8,128)(2,1)}), bf16[80,2,32,8,128]{4,3,2,1,0:T(8,128)(2,1)}, u32[]{:S(2)}, u32[]{:S(2)}) async-start(bf16[80,2,32,8,128]{4,3,2,1,0:T(8,128)(2,1)} %shard_map.167), calls=%async_computation.1 | async-start | bytes 20971520 | tf_op jit(solution)/shard_map/all_to_all | solution.py:393
  384.4 5.7 copy-start.21
  390.4 6.2 copy-start.5
  519.4 132.0 %all-to-all-start = ((bf16[88,2,32,8,128]{4,3,2,1,0:T(8,128)(2,1)}), bf16[88,2,32,8,128]{4,3,2,1,0:T(8,128)(2,1)}, u32[]{:S(2)}, u32[]{:S(2)}) async-start(bf16[88,2,32,8,128]{4,3,2,1,0:T(8,128)(2,1)} %shard_map.166), calls=%async_computation | async-start | bytes 23068672 | tf_op jit(solution)/shard_map/all_to_all | solution.py:393
  651.4 188.4 %all-to-all-start.4 = ((bf16[128,2,32,8,128]{4,3,2,1,0:T(8,128)(2,1)}), bf16[128,2,32,8,128]{4,3,2,1,0:T(8,128)(2,1)}, u32[]{:S(2)}, u32[]{:S(2)}) async-start(bf16[128,2,32,8,128]{4,3,2,1,0:T(8,128)(2,1)} %shard_map.174), calls=%async_computation.4 | async-start | bytes 33554432 | tf_op jit(solution)/shard_map/all_to_all | solution.py:393
  661.9 181.7 %copy-start.12 = (bf16[48,1024]{1,0:T(8,128)(2,1)S(1)}, bf16[48,1024]{1,0:T(8,128)(2,1)}, u32[]{:S(2)}) copy-start(bf16[48,1024]{1,0:T(8,128)(2,1)} %copy-done.11) | copy-start | bytes 294916
  661.9 181.7 %copy-start.14 = (bf16[48,1024]{1,0:T(8,128)(2,1)S(1)}, bf16[48,1024]{1,0:T(8,128)(2,1)}, u32[]{:S(2)}) copy-start(bf16[48,1024]{1,0:T(8,128)(2,1)} %copy-done.13) | copy-start | bytes 294916
  662.0 181.7 %copy-start.8 = (bf16[48,1024]{1,0:T(8,128)(2,1)S(1)}, bf16[48,1024]{1,0:T(8,128)(2,1)}, u32[]{:S(2)}) copy-start(bf16[48,1024]{1,0:T(8,128)(2,1)} %copy-done.7) | copy-start | bytes 294916
  662.0 181.7 %copy-start.10 = (bf16[48,1024]{1,0:T(8,128)(2,1)S(1)}, bf16[48,1024]{1,0:T(8,128)(2,1)}, u32[]{:S(2)}) copy-start(bf16[48,1024]{1,0:T(8,128)(2,1)} %copy-done.9) | copy-start | bytes 294916
  662.0 182.7 %copy-start.18 = (s32[10,3,144]{2,1,0:T(4,128)S(1)}, s32[10,3,144]{2,1,0:T(4,128)}, u32[]{:S(2)}) copy-start(s32[10,3,144]{2,1,0:T(4,128)} %copy-done.17) | copy-start | bytes 51844
  839.8 110.4 %all-to-all-start.3 = ((bf16[64,2,32,8,128]{4,3,2,1,0:T(8,128)(2,1)}), bf16[64,2,32,8,128]{4,3,2,1,0:T(8,128)(2,1)}, u32[]{:S(2)}, u32[]{:S(2)}) async-start(bf16[64,2,32,8,128]{4,3,2,1,0:T(8,128)(2,1)} %shard_map.173), calls=%async_computation.3 | async-start | bytes 16777216 | tf_op jit(solution)/shard_map/all_to_all | solution.py:393
  843.6 107.7 %all-gather.2.cloned.1.call-start = ((), (), s32[]{:S(2)}) async-start(), calls=%async_computation.5 | async-start | bytes 3538944 | tf_op jit(solution)/shard_map/all_gather | solution.py:480
  866.1 22.4 %copy-start.19 = (s32[384]{0:T(512)S(1)}, s32[384]{0:T(512)}, u32[]{:S(2)}) copy-start(s32[384]{0:T(512)} %param.29) | copy-start | bytes 4612
  866.1 22.6 %copy-start.25 = (s32[192]{0:T(256)S(1)}, s32[192]{0:T(256)}, u32[]{:S(2)}) copy-start(s32[192]{0:T(256)} %param.27) | copy-start | bytes 2308
  866.1 22.7 %copy-start.24 = (s32[192]{0:T(256)S(1)}, s32[192]{0:T(256)}, u32[]{:S(2)}) copy-start(s32[192]{0:T(256)} %param.26) | copy-start | bytes 2308
  (8 other events, 8.1 us)
Sparse Core Ops, SparseCore 0:
  846.2 69.0 all-gather.1

commit v2 on v1

--- a/solution.py
+++ b/solution.py
@@ -18,7 +18,7 @@
 DEPTH = 6
 RING = 16
 LAG = 8
-CHUNKS = ((0, 0, 3), (0, 3, 13), (0, 13, 24), (1, 0, 16), (1, 16, 24))
+CHUNKS = ((0, 0, 3), (0, 3, 10), (0, 10, 24), (1, 0, 6), (1, 6, 16), (1, 16, 24))
 
 
 def peers():
@@ -40,45 +40,47 @@
     pl.semaphore_wait(barrier, len(others))
 
 
-def gather_kernel(x_ref, out_ref, local_sem, send_sems, recv_sems):
+def gather_kernel(many, *refs):
+    x_refs, out_refs = refs[:many], refs[many:2 * many]
+    local_sems, send_sems, recv_sems = refs[2 * many:]
     rep, me, core, _, partner, chips = peers()
     same = [c * 2 + core for c in chips]
     meet(rep, same + [partner])
-    own = pltpu.make_async_copy(x_ref, out_ref.at[me], local_sem)
-
-    def remote(src, dst_at, k, dev):
-        return pltpu.make_async_remote_copy(src_ref=src, dst_ref=out_ref.at[dst_at], send_sem=send_sems.at[k], recv_sem=recv_sems.at[k], device_id=(rep, dev), device_id_type=MESH)
-
-    across = [remote(x_ref, me, k, same[k]) for k in (2, 0, 1)]
-    for copy in across:
+
+    def remote(a, src, dst_at, k, dev):
+        return pltpu.make_async_remote_copy(src_ref=src, dst_ref=out_refs[a].at[dst_at], send_sem=send_sems.at[a, k], recv_sem=recv_sems.at[a, k], device_id=(rep, dev), device_id_type=MESH)
+
+    across = [remote(a, x_refs[a], me, k, same[k]) for a in range(many) for k in (2, 0, 1)]
+    to_partner = [remote(a, x_refs[a], me, 3, partner) for a in range(many)]
+    own = [pltpu.make_async_copy(x_refs[a], out_refs[a].at[me], local_sems.at[a]) for a in range(many)]
+    for copy in across + to_partner + own:
         copy.start()
-    to_partner = remote(x_ref, me, 3, partner)
-    to_partner.start()
-    own.start()
     forwards = []
-    for k in (0, 1, 2):
-        remote(x_ref, me, k, same[k]).wait_recv()
-        forward = remote(out_ref.at[same[k]], same[k], 4 + k, partner)
-        forward.start()
-        forwards.append(forward)
-    own.wait()
+    for a in range(many):
+        for k in (2, 0, 1):
+            remote(a, x_refs[a], me, k, same[k]).wait_recv()
+            forward = remote(a, out_refs[a].at[same[k]], same[k], 4 + k, partner)
+            forward.start()
+            forwards.append(forward)
+    for copy in own:
+        copy.wait()
     for copy in across:
         copy.wait_send()
-    to_partner.wait()
-    for forward in forwards:
-        forward.wait()
-
-
-def gather_rows(x, collective_id, groups):
-    return pl.pallas_call(
-        gather_kernel,
-        out_shape=jax.ShapeDtypeStruct((groups,) + x.shape, x.dtype),
-        in_specs=[VMEM],
-        out_specs=ANY,
-        scratch_shapes=[pltpu.SemaphoreType.DMA, pltpu.SemaphoreType.DMA((7,)), pltpu.SemaphoreType.DMA((7,))],
+    for copy in to_partner + forwards:
+        copy.wait()
+
+
+def gather_rows(arrays, collective_id, groups):
+    many = len(arrays)
+    return pl.pallas_call(
+        functools.partial(gather_kernel, many),
+        out_shape=tuple(jax.ShapeDtypeStruct((groups,) + x.shape, x.dtype) for x in arrays),
+        in_specs=[VMEM] * many,
+        out_specs=(ANY,) * many,
+        scratch_shapes=[pltpu.SemaphoreType.DMA((many,)), pltpu.SemaphoreType.DMA((many, 7)), pltpu.SemaphoreType.DMA((many, 7))],
         compiler_params=pltpu.CompilerParams(collective_id=collective_id, has_side_effects=True),
         name='gather_rows',
-    )(x)
+    )(*arrays)
 
 
 def swap_kernel(o_ref, s_ref, o_out, s_out, send_sems, recv_sems):
@@ -240,12 +242,14 @@
     )(lists, q_all, k_pool, v_pool)
 
 
-def patch_kernel(list_ref, rows_ref, k_in, v_in, k_out, v_out, sem):
+def patch_kernel(n_layers, list_ref, *refs):
+    rows_refs = refs[:n_layers]
+    k_out, v_out, sem = refs[n_layers + 2:]
     many = list_ref[3, 0]
 
     def copies(i):
         row, slot, offset = list_ref[0, i], list_ref[1, i], list_ref[2, i]
-        return [pltpu.make_async_copy(rows_ref.at[row, kind], ref.at[slot, :, offset], sem) for kind, ref in ((0, k_out), (1, v_out))]
+        return [pltpu.make_async_copy(rows_refs[layer].at[row, kind], ref.at[slot, layer, offset], sem) for layer in range(n_layers) for kind, ref in ((0, k_out), (1, v_out))]
 
     def start(i, carry):
         for copy in copies(i):
@@ -262,15 +266,16 @@
 
 
 def patch_pools(writes, rows, k_pool, v_pool):
-    return pl.pallas_call(
-        patch_kernel,
+    n_layers = len(rows)
+    return pl.pallas_call(
+        functools.partial(patch_kernel, n_layers),
         out_shape=(jax.ShapeDtypeStruct(k_pool.shape, k_pool.dtype), jax.ShapeDtypeStruct(v_pool.shape, v_pool.dtype)),
-        in_specs=[SMEM, VMEM, ANY, ANY],
+        in_specs=[SMEM] + [VMEM] * n_layers + [ANY, ANY],
         out_specs=(ANY, ANY),
         scratch_shapes=[pltpu.SemaphoreType.DMA],
-        input_output_aliases={2: 0, 3: 1},
+        input_output_aliases={n_layers + 1: 0, n_layers + 2: 1},
         name='patch_pools',
-    )(writes, rows, k_pool, v_pool)
+    )(writes, *rows, k_pool, v_pool)
 
 
 def move_kernel(list_ref, src_ref, *refs):
@@ -380,17 +385,15 @@
         pools = (k_pool, v_pool)
         received = [None] * len(CHUNKS)
 
-        def pack(c, after=None):
+        def pack(c):
             pool, low, high = CHUNKS[c]
-            moves = plan[2 * c]
-            if after is not None:
-                moves, _ = lax.optimization_barrier((moves, after))
-            return move_pages(moves, pools[pool], (groups * (high - low),) + k_pool.shape[1:])
-
-        def send(c, pages, after=None):
-            if after is not None:
-                pages, _ = lax.optimization_barrier((pages, after))
-            received[c] = lax.all_to_all(pages, 'kv', 0, 0, tiled=True)
+            return move_pages(plan[2 * c], pools[pool], (groups * (high - low),) + k_pool.shape[1:])
+
+        def send(c):
+            received[c] = lax.all_to_all(pack(c), 'kv', 0, 0, tiled=True)
+
+        for c in range(len(CHUNKS)):
+            send(c)
 
         page_slot = old_table.reshape(-1) - slot_base
         here = (page_slot >= 0) & (page_slot < slots_dev)
@@ -422,17 +425,17 @@
         def split(stats):
             return stats[..., :lanes], stats[..., lanes:]
 
-        send(0, pack(0))
         hidden = embeds.transpose(1, 0, 2).reshape(rows, d_model)
         new_rows = []
         for layer in range(n_layers):
             query = dot(hidden, w_query[layer]).astype(jnp.bfloat16).reshape(seq_dev, lanes, head_dim)
             k_new = dot(hidden, w_key[layer]).astype(jnp.bfloat16).reshape(seq_dev, n_steps, kv_heads, head_dim)
             v_new = dot(hidden, w_value[layer]).astype(jnp.bfloat16).reshape(seq_dev, n_steps, kv_heads, head_dim)
-            new_rows.append(jnp.stack([k_new, v_new], axis=2))
-
-            packed = pack(layer + 1, query)
-            q_all = gather_rows(query, 3 * layer, groups).reshape(n_batch, lanes, head_dim)
+            rows_own = jnp.stack([k_new, v_new], axis=2)
+
+            q_all, rows_all = gather_rows([query, rows_own], 3 * layer, groups)
+            q_all = q_all.reshape(n_batch, lanes, head_dim)
+            new_rows.append(rows_all.reshape(n_batch * n_steps, 2, kv_heads, head_dim))
             o_part, m_part, l_part = attend_pages(lists, q_all, k_pages, v_pages, layer, kv_heads, scale)
             stats = jnp.concatenate([m_part.T[:n_batch], l_part.T[:n_batch]], axis=1).reshape(groups, seq_dev, 2 * lanes)
             o_part = o_part.reshape(groups, seq_dev, lanes, head_dim)
@@ -450,7 +453,6 @@
             s_chip = jnp.concatenate([m_chip, l_a * f_a + l_b * f_b], axis=-1)
 
             o_far, s_far = home_partials(o_chip, s_chip, 3 * layer + 2)
-            send(layer + 1, packed, o_far)
             o_near = lax.dynamic_index_in_dim(o_chip, chip, 0, keepdims=False)
             m_near, l_near = split(lax.dynamic_index_in_dim(s_chip, chip, 0, keepdims=False))
             m_far, l_far = split(s_far)
@@ -476,18 +478,13 @@
             inner = jax.nn.gelu(dot(mixed, w_up[layer])).astype(jnp.bfloat16)
             hidden = (mixed.astype(jnp.float32) + dot(inner, w_down[layer])).astype(jnp.bfloat16)
 
-        rows_here = jnp.stack(new_rows, axis=3)
-        rows_all = lax.all_gather(rows_here, 'kv', axis=0, tiled=True).reshape(n_batch * n_steps, 2, n_layers, kv_heads, head_dim)
-
-        for c in range(n_layers + 1, len(CHUNKS)):
-            send(c, pack(c, hidden))
         slot_ids = jnp.arange(slots_dev, dtype=jnp.int32)
         every = jnp.stack([slot_ids, slot_ids, jnp.full((slots_dev,), slots_dev, jnp.int32)])
         every, takes, _ = lax.optimization_barrier((every, plan[1::2], hidden))
         outs = [move_pages(every, pool, pool.shape) for pool in pools]
         for c, (pool, low, high) in enumerate(CHUNKS):
             outs[pool] = move_pages(takes[c], received[c], outs[pool])
-        k_out, v_out = patch_pools(writes, rows_all, *outs)
+        k_out, v_out = patch_pools(writes, new_rows, *outs)
 
         home_done = lax.dynamic_slice(finished, (my_dev * seq_dev,), (seq_dev,))
         hidden = hidden.reshape(seq_dev, n_steps, d_model)

time: 974 us -> 787 us (0.81)
  the two profiles are of different devices: /device:TPU:0 before, /device:TPU:4 now
where the time goes in v2:
time: 787 us; the launch traced here: 777 us
  Pallas kernels  411 us (52%)
  matrix products  230 us (29%)
  starting transfers between devices  47.1 us (6%)
  other arithmetic  35 us (4%)
  waiting for transfers between devices  34.4 us (4%)
  local copies, waits for them, and re-layouts  18.1 us (2%)
    dot_general x12, matrix products, dot(): return jnp.dot(a, b, preferred_element_type=jnp.float32)  229 us
    pallas_call x2, Pallas kernels, home_partials(): pl.pallas_call(home_kernel, out_shape=(jax.ShapeDtypeStruct((3,) + o.shap...  129 us
    pallas_call x2, Pallas kernels, gather_rows(): pl.pallas_call(functools.partial(gather_kernel, many), out_shape=tuple((j...  88.9 us
    pallas_call x14, Pallas kernels, move_pages(): pl.pallas_call(move_kernel, out_shape=jax.ShapeDtypeStruct(shape, src.dty...  84.2 us
    pallas_call x2, Pallas kernels, swap_partials(): pl.pallas_call(swap_kernel, out_shape=(jax.ShapeDtypeStruct((4,) + o.shap...  64.1 us
    all_to_all x6, starting transfers between devices, send(): received[c] = lax.all_to_all(pack(c), 'kv', 0, 0, tiled=True)  47.1 us
    pallas_call x2, Pallas kernels, attend_pages(): pl.pallas_call(functools.partial(attend_kernel, layer, n_seq, heads, scal...  39.2 us
    all_to_all x6, waiting for transfers between devices, send(): received[c] = lax.all_to_all(pack(c), 'kv', 0, 0, tiled=True)  34.4 us
  transfers between devices with their start and end apart: 6, of which 2 were waited for; matrix products, arithmetic and copies ran while one was open for 36% of the time, Pallas kernels for 51%

profile of v2, /device:TPU:4, one launch (start us, length us, event | category | flops | bytes accessed | tf_op | source)
XLA Modules:
  0.0 777.2 jit_solution(14746944850814790671)
XLA Ops:
  23.3 13.6 %fusion.60 = bf16[48,4096]{1,0:T(8,128)(2,1)S(1)} fusion(bf16[48,4096]{1,0:T(8,128)(2,1)S(1)} %reshape.811, bf16[2,4096,4096]{2,1,0:T(8,128)(2,1)} %param.16), kind=kOutput, calls=%fused_computation.44 | convolution fusion | flops 1610809344 | bytes 34340864 | tf_op jit(solution)/shard_map/dot_general | solution.py:423
  39.2 35.9 %gather_rows.2 = (bf16[8,24,64,128]{3,2,1,0:T(8,128)(2,1)}, bf16[8,24,2,2,8,128]{5,4,3,2,1,0:T(8,128)(2,1)}) custom-call(bf16[24,64,128]{2,1,0:T(8,128)(2,1)} %reshape.812.refs_0_, bf16[24,2,2,8,128]{4,3,2,1,0:T(8,128)(2,1)} %pad_maximum_fusion.1.refs_1_), custom_call_target="tpu_custom_call" | custom-call | tf_op jit(solution)/shard_map/gather_rows/pallas_call | solution.py:75
  76.7 8.6 %all-to-all-start.5 = ((bf16[48,2,32,8,128]{4,3,2,1,0:T(8,128)(2,1)}), bf16[48,2,32,8,128]{4,3,2,1,0:T(8,128)(2,1)}, u32[]{:S(2)}, u32[]{:S(2)}) async-start(bf16[48,2,32,8,128]{4,3,2,1,0:T(8,128)(2,1)} %shard_map.175), calls=%async_computation.5 | async-start | bytes 12582912 | tf_op jit(solution)/shard_map/all_to_all | solution.py:393
  85.4 19.7 %attend_pages.2 = (f32[192,64,128]{2,1,0:T(8,128)}, f32[64,256]{1,0:T(8,128)S(1)}, f32[64,256]{1,0:T(8,128)S(1)}) custom-call(s32[4,160]{1,0:T(4,128)S(1)} %add_bitcast_fusion.1.list_ref, bf16[192,64,128]{2,1,0:T(8,128)(2,1)S(1)} %bitcast.306, bf16[144,2,256,128]{3,2,1,0:T(8,128)(2,1)} %bitcast.310, bf16[144,2,256,128]{3,2,1,0:T(8,128)(2,1)} %bitcast.308), custom_call_target="tpu_custom_call" | custom-call | flops 40000000000 | bytes 30000000 | tf_op jit(solution)/shard_map/attend_pages/pallas_call | solution.py:223
  108.6 32.1 %swap_partials.2 = (f32[4,24,64,128]{3,2,1,0:T(8,128)}, f32[4,24,128]{2,1,0:T(8,128)}) custom-call(f32[8,24,64,128]{3,2,1,0:T(8,128)} %bitcast.312, f32[8,24,128]{2,1,0:T(8,128)} %bitcast.325), custom_call_target="tpu_custom_call" | custom-call | tf_op jit(solution)/shard_map/swap_partials/pallas_call | solution.py:101
  148.5 41.4 %home_partials.2 = (f32[3,24,64,128]{3,2,1,0:T(8,128)}, f32[3,24,128]{2,1,0:T(8,128)}) custom-call(f32[4,24,64,128]{3,2,1,0:T(8,128)} %fusion.67.o_ref, f32[4,24,128]{2,1,0:T(8,128)} %pad_maximum_fusion.5.s_ref), custom_call_target="tpu_custom_call" | custom-call | tf_op jit(solution)/shard_map/home_partials/pallas_call | solution.py:127
  196.6 9.7 %all-to-all-start.1 = ((bf16[56,2,32,8,128]{4,3,2,1,0:T(8,128)(2,1)}), bf16[56,2,32,8,128]{4,3,2,1,0:T(8,128)(2,1)}, u32[]{:S(2)}, u32[]{:S(2)}) async-start(bf16[56,2,32,8,128]{4,3,2,1,0:T(8,128)(2,1)} %shard_map.167), calls=%async_computation.1 | async-start | bytes 14680064 | tf_op jit(solution)/shard_map/all_to_all | solution.py:393
  206.3 13.7 %fusion.57 = bf16[48,4096]{1,0:T(8,128)(2,1)S(1)} fusion(bf16[48,4096]{1,0:T(8,128)(2,1)S(1)} %convert_element_type.187, bf16[2,4096,4096]{2,1,0:T(8,128)(2,1)} %param.19, bf16[48,4096]{1,0:T(8,128)(2,1)S(1)} %copy-done.9), kind=kOutput, calls=%fused_computation.43 | convolution fusion | flops 1611202560 | bytes 34734080 | tf_op jit(solution)/shard_map/dot_general | solution.py:423
  221.0 38.8 %fusion.77.clone.5 = bf16[48,14336]{1,0:T(8,128)(2,1)S(1)} fusion(bf16[48,4096]{1,0:T(8,128)(2,1)S(1)} %fusion.57, bf16[2,4096,14336]{2,1,0:T(8,128)(2,1)} %param.20), kind=kOutput, calls=%fused_computation.59.clone.clone.clone.2 | convolution fusion | flops 5643337728 | bytes 119209984 | tf_op jit(solution)/shard_map/dot_general | solution.py:423
  259.8 27.9 %all-to-all-done.1.src_ref = bf16[56,2,32,8,128]{4,3,2,1,0:T(8,128)(2,1)} async-done(((bf16[56,2,32,8,128]{4,3,2,1,0:T(8,128)(2,1)}), bf16[56,2,32,8,128]{4,3,2,1,0:T(8,128)(2,1)}, u32[]{:S(2)}, u32[]{:S(2)}) %all-to-all-start.1) | async-done | bytes 7340064 | tf_op jit(solution)/shard_map/all_to_all | solution.py:393
  293.0 38.4 %fusion.51 = bf16[48,4096]{1,0:T(8,128)(2,1)S(1)} fusion(bf16[2,14336,4096]{2,1,0:T(8,128)(2,1)} %param.21, bf16[48,4096]{1,0:T(8,128)(2,1)S(1)} %fusion.57, bf16[48,14336]{1,0:T(8,128)(2,1)S(1)} %fusion.77.clone.5), kind=kOutput, calls=%fused_computation.41 | convolution fusion | flops 5637734400 | bytes 119603200 | tf_op jit(solution)/shard_map/dot_general | solution.py:423
  331.4 13.8 %fusion.63 = bf16[48,4096]{1,0:T(8,128)(2,1)S(1)} fusion(bf16[48,4096]{1,0:T(8,128)(2,1)S(1)} %fusion.51, bf16[2,4096,4096]{2,1,0:T(8,128)(2,1)} %param.16), kind=kOutput, calls=%fused_computation.45 | convolution fusion | flops 1610809344 | bytes 34340864 | tf_op jit(solution)/shard_map/dot_general | solution.py:423
  360.0 53.0 %gather_rows.3 = (bf16[8,24,64,128]{3,2,1,0:T(8,128)(2,1)}, bf16[8,24,2,2,8,128]{5,4,3,2,1,0:T(8,128)(2,1)}) custom-call(bf16[24,64,128]{2,1,0:T(8,128)(2,1)} %reshape.821.refs_0_, bf16[24,2,2,8,128]{4,3,2,1,0:T(8,128)(2,1)} %pad_maximum_fusion.2.refs_1_), custom_call_target="tpu_custom_call" | custom-call | tf_op jit(solution)/shard_map/gather_rows/pallas_call | solution.py:75
  418.3 19.4 %attend_pages.3 = (f32[192,64,128]{2,1,0:T(8,128)}, f32[64,256]{1,0:T(8,128)S(1)}, f32[64,256]{1,0:T(8,128)S(1)}) custom-call(s32[4,160]{1,0:T(4,128)S(1)} %add_bitcast_fusion.1.list_ref, bf16[192,64,128]{2,1,0:T(8,128)(2,1)S(1)} %bitcast.307, bf16[144,2,256,128]{3,2,1,0:T(8,128)(2,1)} %bitcast.311, bf16[144,2,256,128]{3,2,1,0:T(8,128)(2,1)} %bitcast.309), custom_call_target="tpu_custom_call" | custom-call | flops 40000000000 | bytes 30000000 | tf_op jit(solution)/shard_map/attend_pages/pallas_call | solution.py:223
  440.7 32.1 %swap_partials.3 = (f32[4,24,64,128]{3,2,1,0:T(8,128)}, f32[4,24,128]{2,1,0:T(8,128)}) custom-call(f32[8,24,64,128]{3,2,1,0:T(8,128)} %bitcast.314, f32[8,24,128]{2,1,0:T(8,128)} %bitcast.327), custom_call_target="tpu_custom_call" | custom-call | tf_op jit(solution)/shard_map/swap_partials/pallas_call | solution.py:101
  480.6 87.2 %home_partials.3 = (f32[3,24,64,128]{3,2,1,0:T(8,128)}, f32[3,24,128]{2,1,0:T(8,128)}) custom-call(f32[4,24,64,128]{3,2,1,0:T(8,128)} %fusion.66.o_ref, f32[4,24,128]{2,1,0:T(8,128)} %pad_maximum_fusion.6.s_ref), custom_call_target="tpu_custom_call" | custom-call | tf_op jit(solution)/shard_map/home_partials/pallas_call | solution.py:127
  575.3 13.7 %fusion.54 = bf16[48,4096]{1,0:T(8,128)(2,1)S(1)} fusion(bf16[48,4096]{1,0:T(8,128)(2,1)S(1)} %convert_element_type.203, bf16[2,4096,4096]{2,1,0:T(8,128)(2,1)} %param.19, bf16[48,4096]{1,0:T(8,128)(2,1)S(1)} %copy-done.23), kind=kOutput, calls=%fused_computation.42 | convolution fusion | flops 1611202560 | bytes 34734080 | tf_op jit(solution)/shard_map/dot_general | solution.py:423
  588.9 12.9 %all-to-all-start = ((bf16[112,2,32,8,128]{4,3,2,1,0:T(8,128)(2,1)}), bf16[112,2,32,8,128]{4,3,2,1,0:T(8,128)(2,1)}, u32[]{:S(2)}, u32[]{:S(2)}) async-start(bf16[112,2,32,8,128]{4,3,2,1,0:T(8,128)(2,1)} %shard_map.166), calls=%async_computation | async-start | bytes 29360128 | tf_op jit(solution)/shard_map/all_to_all | solution.py:393
  601.8 38.8 %fusion.91.clone.5 = bf16[48,14336]{1,0:T(8,128)(2,1)S(1)} fusion(bf16[48,4096]{1,0:T(8,128)(2,1)S(1)} %fusion.54, bf16[2,4096,14336]{2,1,0:T(8,128)(2,1)} %param.20), kind=kOutput, calls=%fused_computation.67.clone.clone.clone.2 | convolution fusion | flops 5643337728 | bytes 119209984 | tf_op jit(solution)/shard_map/dot_general | solution.py:423
  640.6 38.4 %fusion.48 = bf16[48,4096]{1,0:T(8,128)(2,1)S(1)} fusion(bf16[2,14336,4096]{2,1,0:T(8,128)(2,1)} %param.21, bf16[48,4096]{1,0:T(8,128)(2,1)S(1)} %fusion.54, bf16[48,14336]{1,0:T(8,128)(2,1)S(1)} %fusion.91.clone.5), kind=kOutput, calls=%fused_computation.40 | convolution fusion | flops 5637734400 | bytes 119603200 | tf_op jit(solution)/shard_map/dot_general | solution.py:423
  679.0 20.6 %shard_map.176.refs_0_ = bf16[144,2,32,8,128]{4,3,2,1,0:T(8,128)(2,1)} custom-call(s32[3,144]{1,0:T(4,128)} %add_add_fusion.list_ref, bf16[144,2,32,8,128]{4,3,2,1,0:T(8,128)(2,1)} %src_ref.15), custom_call_target="tpu_custom_call" | custom-call | tf_op jit(solution)/shard_map/pallas_call | solution.py:323
  699.6 21.0 %shard_map.169.refs_0_ = bf16[144,2,32,8,128]{4,3,2,1,0:T(8,128)(2,1)} custom-call(s32[3,144]{1,0:T(4,128)} %add_add_fusion.list_ref, bf16[144,2,32,8,128]{4,3,2,1,0:T(8,128)(2,1)} %src_ref.11), custom_call_target="tpu_custom_call" | custom-call | tf_op jit(solution)/shard_map/pallas_call | solution.py:323
  742.3 7.1 shard_map.178.refs_0_
  761.9 9.2 %shard_map.172.refs_2_ = bf16[144,2,32,8,128]{4,3,2,1,0:T(8,128)(2,1)} custom-call(s32[3,144]{1,0:T(4,128)} %get-tuple-element.114.list_ref, bf16[112,2,32,8,128]{4,3,2,1,0:T(8,128)(2,1)} %all-to-all-done.src_ref, bf16[144,2,32,8,128]{4,3,2,1,0:T(8,128)(2,1)} %shard_map.171.refs_0_), custom_call_target="tpu_custom_call", output_to_operand_aliasing={{}: (2, {})} | custom-call | tf_op jit(solution)/shard_map/pallas_call | solution.py:323
  (232 shorter events, 128.1 us)
Async XLA Ops:
  5.9 5.3 copy-start.18
  5.9 5.3 copy-start.19
  5.9 6.6 copy-start.7
  5.9 70.8 %all-to-all-start.2 = ((bf16[24,2,32,8,128]{4,3,2,1,0:T(8,128)(2,1)}), bf16[24,2,32,8,128]{4,3,2,1,0:T(8,128)(2,1)}, u32[]{:S(2)}, u32[]{:S(2)}) async-start(bf16[24,2,32,8,128]{4,3,2,1,0:T(8,128)(2,1)} %shard_map.168), calls=%async_computation.2 | async-start | bytes 6291456 | tf_op jit(solution)/shard_map/all_to_all | solution.py:393
  13.1 10.1 %copy-start.8 = (bf16[48,4096]{1,0:T(8,128)(2,1)}, bf16[48,4096]{1,0:T(8,128)(2,1)S(1)}, u32[]{:S(2)}) copy-start(bf16[48,4096]{1,0:T(8,128)(2,1)S(1)} %reshape.811) | copy-start | bytes 1179652
  36.9 39.2 %copy-start.4 = (bf16[48,4096]{1,0:T(8,128)(2,1)}, bf16[48,4096]{1,0:T(8,128)(2,1)S(1)}, u32[]{:S(2)}) copy-start(bf16[48,4096]{1,0:T(8,128)(2,1)S(1)} %fusion.60) | copy-start | bytes 1179652
  76.7 8.6 %copy-start = (bf16[8,24,64,128]{3,2,1,0:T(8,128)(2,1)S(1)}, bf16[8,24,64,128]{3,2,1,0:T(8,128)(2,1)}, u32[]{:S(2)}) copy-start(bf16[8,24,64,128]{3,2,1,0:T(8,128)(2,1)} %get-tuple-element.25) | copy-start | bytes 9437188
  76.7 119.8 %all-to-all-start.5 = ((bf16[48,2,32,8,128]{4,3,2,1,0:T(8,128)(2,1)}), bf16[48,2,32,8,128]{4,3,2,1,0:T(8,128)(2,1)}, u32[]{:S(2)}, u32[]{:S(2)}) async-start(bf16[48,2,32,8,128]{4,3,2,1,0:T(8,128)(2,1)} %shard_map.175), calls=%async_computation.5 | async-start | bytes 12582912 | tf_op jit(solution)/shard_map/all_to_all | solution.py:393
  107.7 83.5 %copy-start.16 = (pred[2,2]{1,0:T(4,128)(4,1)}, pred[2,2]{1,0:T(4,128)(4,1)S(1)}, u32[]{:S(2)}) copy-start(pred[2,2]{1,0:T(4,128)(4,1)S(1)} %iota_compare_fusion.14) | copy-start | bytes 16
  108.6 32.1 %copy-start.5 = (f32[192,128]{1,0:T(8,128)S(1)}, f32[192,128]{1,0:T(8,128)}, u32[]{:S(2)}) copy-start(f32[192,128]{1,0:T(8,128)} %copy.77) | copy-start | bytes 294916
  196.5 9.7 %copy-start.9 = (bf16[48,4096]{1,0:T(8,128)(2,1)S(1)}, bf16[48,4096]{1,0:T(8,128)(2,1)}, u32[]{:S(2)}) copy-start(bf16[48,4096]{1,0:T(8,128)(2,1)} %copy-done.8) | copy-start | bytes 1179652
  196.6 91.1 %all-to-all-start.1 = ((bf16[56,2,32,8,128]{4,3,2,1,0:T(8,128)(2,1)}), bf16[56,2,32,8,128]{4,3,2,1,0:T(8,128)(2,1)}, u32[]{:S(2)}, u32[]{:S(2)}) async-start(bf16[56,2,32,8,128]{4,3,2,1,0:T(8,128)(2,1)} %shard_map.167), calls=%async_computation.1 | async-start | bytes 14680064 | tf_op jit(solution)/shard_map/all_to_all | solution.py:393
  287.7 125.3 %all-to-all-start.3 = ((bf16[64,2,32,8,128]{4,3,2,1,0:T(8,128)(2,1)}), bf16[64,2,32,8,128]{4,3,2,1,0:T(8,128)(2,1)}, u32[]{:S(2)}, u32[]{:S(2)}) async-start(bf16[64,2,32,8,128]{4,3,2,1,0:T(8,128)(2,1)} %shard_map.173), calls=%async_computation.3 | async-start | bytes 16777216 | tf_op jit(solution)/shard_map/all_to_all | solution.py:393
  331.4 21.8 %copy-start.22 = (bf16[48,4096]{1,0:T(8,128)(2,1)}, bf16[48,4096]{1,0:T(8,128)(2,1)S(1)}, u32[]{:S(2)}) copy-start(bf16[48,4096]{1,0:T(8,128)(2,1)S(1)} %fusion.51) | copy-start | bytes 1179652
  331.4 16.2 %copy-start.13 = (s32[12,3,144]{2,1,0:T(4,128)S(1)}, s32[12,3,144]{2,1,0:T(4,128)}, u32[]{:S(2)}) copy-start(s32[12,3,144]{2,1,0:T(4,128)} %copy-done.12) | copy-start | bytes 62212
  413.0 5.3 copy-start.1
  413.0 175.9 %all-to-all-start.4 = ((bf16[80,2,32,8,128]{4,3,2,1,0:T(8,128)(2,1)}), bf16[80,2,32,8,128]{4,3,2,1,0:T(8,128)(2,1)}, u32[]{:S(2)}, u32[]{:S(2)}) async-start(bf16[80,2,32,8,128]{4,3,2,1,0:T(8,128)(2,1)} %shard_map.174), calls=%async_computation.4 | async-start | bytes 20971520 | tf_op jit(solution)/shard_map/all_to_all | solution.py:393
  437.7 2.7 copy-start.17
  440.7 32.1 %copy-start.6 = (f32[192,128]{1,0:T(8,128)S(1)}, f32[192,128]{1,0:T(8,128)}, u32[]{:S(2)}) copy-start(f32[192,128]{1,0:T(8,128)} %copy.90) | copy-start | bytes 294916
  588.9 173.0 %all-to-all-start = ((bf16[112,2,32,8,128]{4,3,2,1,0:T(8,128)(2,1)}), bf16[112,2,32,8,128]{4,3,2,1,0:T(8,128)(2,1)}, u32[]{:S(2)}, u32[]{:S(2)}) async-start(bf16[112,2,32,8,128]{4,3,2,1,0:T(8,128)(2,1)} %shard_map.166), calls=%async_computation | async-start | bytes 29360128 | tf_op jit(solution)/shard_map/all_to_all | solution.py:393
  699.6 22.7 %copy-start.15 = (s32[384]{0:T(512)S(1)}, s32[384]{0:T(512)}, u32[]{:S(2)}) copy-start(s32[384]{0:T(512)} %param.29) | copy-start | bytes 4612
  699.6 22.9 %copy-start.21 = (s32[192]{0:T(256)S(1)}, s32[192]{0:T(256)}, u32[]{:S(2)}) copy-start(s32[192]{0:T(256)} %param.27) | copy-start | bytes 2308
  699.6 23.0 %copy-start.20 = (s32[192]{0:T(256)S(1)}, s32[192]{0:T(256)}, u32[]{:S(2)}) copy-start(s32[192]{0:T(256)} %param.26) | copy-start | bytes 2308
  720.6 6.1 copy-start.14
  (6 other events, 12.4 us)

commit v3 on v2

--- a/solution.py
+++ b/solution.py
@@ -16,9 +16,9 @@
 ENTRY_PAD = 160
 GROUP = 4
 DEPTH = 6
-RING = 16
-LAG = 8
-CHUNKS = ((0, 0, 3), (0, 3, 10), (0, 10, 24), (1, 0, 6), (1, 6, 16), (1, 16, 24))
+RING = 48
+LAG = 24
+CHUNKS = ((0, 0, 8), (0, 8, 18), (0, 18, 24), (1, 0, 2), (1, 2, 11), (1, 11, 24))
 
 
 def peers():
@@ -243,13 +243,13 @@
 
 
 def patch_kernel(n_layers, list_ref, *refs):
-    rows_refs = refs[:n_layers]
-    k_out, v_out, sem = refs[n_layers + 2:]
+    rows_refs = refs[:2 * n_layers]
+    k_out, v_out, sem = refs[2 * n_layers + 2:]
     many = list_ref[3, 0]
 
     def copies(i):
         row, slot, offset = list_ref[0, i], list_ref[1, i], list_ref[2, i]
-        return [pltpu.make_async_copy(rows_refs[layer].at[row, kind], ref.at[slot, layer, offset], sem) for layer in range(n_layers) for kind, ref in ((0, k_out), (1, v_out))]
+        return [pltpu.make_async_copy(rows_refs[kind * n_layers + layer].at[row], ref.at[slot, layer, offset], sem) for layer in range(n_layers) for kind, ref in ((0, k_out), (1, v_out))]
 
     def start(i, carry):
         for copy in copies(i):
@@ -266,14 +266,14 @@
 
 
 def patch_pools(writes, rows, k_pool, v_pool):
-    n_layers = len(rows)
+    n_layers = len(rows) // 2
     return pl.pallas_call(
         functools.partial(patch_kernel, n_layers),
         out_shape=(jax.ShapeDtypeStruct(k_pool.shape, k_pool.dtype), jax.ShapeDtypeStruct(v_pool.shape, v_pool.dtype)),
-        in_specs=[SMEM] + [VMEM] * n_layers + [ANY, ANY],
+        in_specs=[SMEM] + [VMEM] * len(rows) + [ANY, ANY],
         out_specs=(ANY, ANY),
         scratch_shapes=[pltpu.SemaphoreType.DMA],
-        input_output_aliases={n_layers + 1: 0, n_layers + 2: 1},
+        input_output_aliases={len(rows) + 1: 0, len(rows) + 2: 1},
         name='patch_pools',
     )(writes, *rows, k_pool, v_pool)
 
@@ -426,16 +426,20 @@
             return stats[..., :lanes], stats[..., lanes:]
 
         hidden = embeds.transpose(1, 0, 2).reshape(rows, d_model)
-        new_rows = []
+        k_rows, v_rows = [], []
         for layer in range(n_layers):
-            query = dot(hidden, w_query[layer]).astype(jnp.bfloat16).reshape(seq_dev, lanes, head_dim)
-            k_new = dot(hidden, w_key[layer]).astype(jnp.bfloat16).reshape(seq_dev, n_steps, kv_heads, head_dim)
-            v_new = dot(hidden, w_value[layer]).astype(jnp.bfloat16).reshape(seq_dev, n_steps, kv_heads, head_dim)
-            rows_own = jnp.stack([k_new, v_new], axis=2)
-
-            q_all, rows_all = gather_rows([query, rows_own], 3 * layer, groups)
-            q_all = q_all.reshape(n_batch, lanes, head_dim)
-            new_rows.append(rows_all.reshape(n_batch * n_steps, 2, kv_heads, head_dim))
+            hidden_all, = gather_rows([hidden], 3 * layer, groups)
+            hidden_all = hidden_all.reshape(groups * rows, d_model)
+            q_all = dot(hidden_all, w_query[layer]).astype(jnp.bfloat16).reshape(n_batch, lanes, head_dim)
+            k_rows.append(dot(hidden_all, w_key[layer]).astype(jnp.bfloat16).reshape(n_batch * n_steps, kv_heads, head_dim))
+            v_rows.append(dot(hidden_all, w_value[layer]).astype(jnp.bfloat16).reshape(n_batch * n_steps, kv_heads, head_dim))
+
+            def mine(values, many):
+                return lax.dynamic_slice_in_dim(values, my_dev * many, many)
+
+            query = mine(q_all, seq_dev)
+            k_new = mine(k_rows[layer], rows)
+            v_new = mine(v_rows[layer], rows)
             o_part, m_part, l_part = attend_pages(lists, q_all, k_pages, v_pages, layer, kv_heads, scale)
             stats = jnp.concatenate([m_part.T[:n_batch], l_part.T[:n_batch]], axis=1).reshape(groups, seq_dev, 2 * lanes)
             o_part = o_part.reshape(groups, seq_dev, lanes, head_dim)
@@ -480,11 +484,10 @@
 
         slot_ids = jnp.arange(slots_dev, dtype=jnp.int32)
         every = jnp.stack([slot_ids, slot_ids, jnp.full((slots_dev,), slots_dev, jnp.int32)])
-        every, takes, _ = lax.optimization_barrier((every, plan[1::2], hidden))
         outs = [move_pages(every, pool, pool.shape) for pool in pools]
         for c, (pool, low, high) in enumerate(CHUNKS):
-            outs[pool] = move_pages(takes[c], received[c], outs[pool])
-        k_out, v_out = patch_pools(writes, new_rows, *outs)
+            outs[pool] = move_pages(plan[2 * c + 1], received[c], outs[pool])
+        k_out, v_out = patch_pools(writes, k_rows + v_rows, *outs)
 
         home_done = lax.dynamic_slice(finished, (my_dev * seq_dev,), (seq_dev,))
         hidden = hidden.reshape(seq_dev, n_steps, d_model)

time: 787 us -> 880 us (1.12)
  the two profiles are of different devices: /device:TPU:4 before, /device:TPU:0 now
where the time goes in v3:
time: 880 us; the launch traced here: 865 us
  Pallas kernels  421 us (48%)
  matrix products  252 us (29%)
  waiting for transfers between devices  103 us (12%)
  other arithmetic  33.7 us (4%)
  local copies, waits for them, and re-layouts  29.2 us (3%)
  starting transfers between devices  24 us (3%)
    dot_general x12, matrix products, dot(): return jnp.dot(a, b, preferred_element_type=jnp.float32)  251 us
    pallas_call x2, Pallas kernels, home_partials(): pl.pallas_call(home_kernel, out_shape=(jax.ShapeDtypeStruct((3,) + o.shap...  160 us
    all_to_all x6, waiting for transfers between devices, send(): received[c] = lax.all_to_all(pack(c), 'kv', 0, 0, tiled=True)  103 us
    pallas_call x2, Pallas kernels, attend_pages(): pl.pallas_call(functools.partial(attend_kernel, layer, n_seq, heads, scal...  90.9 us
    pallas_call x2, Pallas kernels, gather_rows(): pl.pallas_call(functools.partial(gather_kernel, many), out_shape=tuple((j...  82.5 us
    pallas_call x14, Pallas kernels, move_pages(): pl.pallas_call(move_kernel, out_shape=jax.ShapeDtypeStruct(shape, src.dty...  72.4 us
    all_to_all x6, starting transfers between devices, send(): received[c] = lax.all_to_all(pack(c), 'kv', 0, 0, tiled=True)  24 us
  transfers between devices with their start and end apart: 6, of which 2 were waited for; matrix products, arithmetic and copies ran while one was open for 36% of the time, Pallas kernels for 48%

profile of v3, /device:TPU:0, one launch (start us, length us, event | category | flops | bytes accessed | tf_op | source)
XLA Modules:
  0.0 865.3 jit_solution(8579763566335074535)
XLA Ops:
  15.0 42.2 %gather_rows.2 = bf16[8,48,4096]{2,1,0:T(8,128)(2,1)} custom-call(bf16[48,4096]{1,0:T(8,128)(2,1)} %reshape.777.refs_0_), custom_call_target="tpu_custom_call" | custom-call | tf_op jit(solution)/shard_map/gather_rows/pallas_call | solution.py:75
  57.3 21.1 %fusion.36 = bf16[384,4096]{1,0:T(8,128)(2,1)} fusion(bf16[384,4096]{1,0:T(8,128)(2,1)} %bitcast.326, bf16[2,4096,4096]{2,1,0:T(8,128)(2,1)} %param.16), kind=kOutput, calls=%fused_computation.36 | convolution fusion | flops 12886474752 | bytes 39845888 | tf_op jit(solution)/shard_map/dot_general | solution.py:423
  83.7 45.3 %attend_pages.2 = (f32[192,64,128]{2,1,0:T(8,128)}, f32[64,256]{1,0:T(8,128)S(1)}, f32[64,256]{1,0:T(8,128)S(1)}) custom-call(s32[4,160]{1,0:T(4,128)S(1)} %add_bitcast_fusion.1.list_ref, bf16[192,64,128]{2,1,0:T(8,128)(2,1)S(1)} %reshape.779.q_ref, bf16[144,2,256,128]{3,2,1,0:T(8,128)(2,1)} %bitcast.310, bf16[144,2,256,128]{3,2,1,0:T(8,128)(2,1)} %bitcast.312), custom_call_target="tpu_custom_call" | custom-call | flops 40000000000 | bytes 30000000 | tf_op jit(solution)/shard_map/attend_pages/pallas_call | solution.py:223
  150.0 7.9 fusion.127
  168.1 6.3 swap_partials.2
  182.2 72.1 %home_partials.2 = (f32[3,24,64,128]{3,2,1,0:T(8,128)}, f32[3,24,128]{2,1,0:T(8,128)}) custom-call(f32[4,24,64,128]{3,2,1,0:T(8,128)} %fusion.67.o_ref, f32[4,24,128]{2,1,0:T(8,128)} %pad_maximum_fusion.3.s_ref), custom_call_target="tpu_custom_call" | custom-call | tf_op jit(solution)/shard_map/home_partials/pallas_call | solution.py:127
  263.9 13.7 %fusion.63 = bf16[48,4096]{1,0:T(8,128)(2,1)S(1)} fusion(bf16[48,4096]{1,0:T(8,128)(2,1)S(1)} %convert_element_type.127, bf16[2,4096,4096]{2,1,0:T(8,128)(2,1)} %param.19, bf16[48,4096]{1,0:T(8,128)(2,1)S(1)} %copy-done.6), kind=kOutput, calls=%fused_computation.45 | convolution fusion | flops 1611202560 | bytes 34734080 | tf_op jit(solution)/shard_map/dot_general | solution.py:423
  277.6 38.8 %fusion.77.clone.5 = bf16[48,14336]{1,0:T(8,128)(2,1)S(1)} fusion(bf16[48,4096]{1,0:T(8,128)(2,1)S(1)} %fusion.63, bf16[2,4096,14336]{2,1,0:T(8,128)(2,1)} %param.20), kind=kOutput, calls=%fused_computation.59.clone.clone.clone.2 | convolution fusion | flops 5643337728 | bytes 119209984 | tf_op jit(solution)/shard_map/dot_general | solution.py:423
  316.3 41.6 %all-to-all-done.2.src_ref = bf16[64,2,32,8,128]{4,3,2,1,0:T(8,128)(2,1)} async-done(((bf16[64,2,32,8,128]{4,3,2,1,0:T(8,128)(2,1)}), bf16[64,2,32,8,128]{4,3,2,1,0:T(8,128)(2,1)}, u32[]{:S(2)}, u32[]{:S(2)}) %all-to-all-start.2) | async-done | bytes 8388640 | tf_op jit(solution)/shard_map/all_to_all | solution.py:393
  361.7 39.1 %fusion.57.refs_0_ = bf16[48,4096]{1,0:T(8,128)(2,1)} fusion(bf16[2,14336,4096]{2,1,0:T(8,128)(2,1)} %param.21, bf16[48,4096]{1,0:T(8,128)(2,1)S(1)} %fusion.63, bf16[48,14336]{1,0:T(8,128)(2,1)S(1)} %fusion.77.clone.5), kind=kOutput, calls=%fused_computation.43 | convolution fusion | flops 5637734400 | bytes 119603200 | tf_op jit(solution)/shard_map/dot_general | solution.py:423
  401.5 14.9 %shard_map.169.refs_0_ = bf16[144,2,32,8,128]{4,3,2,1,0:T(8,128)(2,1)} custom-call(s32[3,144]{1,0:T(4,128)} %add_add_fusion.list_ref, bf16[144,2,32,8,128]{4,3,2,1,0:T(8,128)(2,1)} %src_ref.11), custom_call_target="tpu_custom_call" | custom-call | tf_op jit(solution)/shard_map/pallas_call | solution.py:323
  416.4 14.9 %shard_map.176.refs_0_ = bf16[144,2,32,8,128]{4,3,2,1,0:T(8,128)(2,1)} custom-call(s32[3,144]{1,0:T(4,128)} %add_add_fusion.list_ref, bf16[144,2,32,8,128]{4,3,2,1,0:T(8,128)(2,1)} %src_ref.15), custom_call_target="tpu_custom_call" | custom-call | tf_op jit(solution)/shard_map/pallas_call | solution.py:323
  432.1 6.2 shard_map.167
  438.3 7.1 shard_map.173
  445.4 40.3 %gather_rows.3 = bf16[8,48,4096]{2,1,0:T(8,128)(2,1)} custom-call(bf16[48,4096]{1,0:T(8,128)(2,1)} %fusion.57.refs_0_), custom_call_target="tpu_custom_call" | custom-call | tf_op jit(solution)/shard_map/gather_rows/pallas_call | solution.py:75
  485.7 7.9 fusion.121
  507.3 20.2 %fusion.39 = bf16[384,4096]{1,0:T(8,128)(2,1)} fusion(bf16[384,4096]{1,0:T(8,128)(2,1)S(1)} %bitcast.331, bf16[2,4096,4096]{2,1,0:T(8,128)(2,1)} %param.16), kind=kOutput, calls=%fused_computation.37 | convolution fusion | flops 12886474752 | bytes 39845888 | tf_op jit(solution)/shard_map/dot_general | solution.py:423
  535.7 45.7 %attend_pages.3 = (f32[192,64,128]{2,1,0:T(8,128)}, f32[64,256]{1,0:T(8,128)S(1)}, f32[64,256]{1,0:T(8,128)S(1)}) custom-call(s32[4,160]{1,0:T(4,128)S(1)} %copy-done.1, bf16[192,64,128]{2,1,0:T(8,128)(2,1)S(1)} %reshape.790.q_ref, bf16[144,2,256,128]{3,2,1,0:T(8,128)(2,1)} %bitcast.311, bf16[144,2,256,128]{3,2,1,0:T(8,128)(2,1)} %bitcast.313), custom_call_target="tpu_custom_call" | custom-call | flops 40000000000 | bytes 30000000 | tf_op jit(solution)/shard_map/attend_pages/pallas_call | solution.py:223
  584.2 6.2 swap_partials.3
  598.2 87.5 %home_partials.3 = (f32[3,24,64,128]{3,2,1,0:T(8,128)}, f32[3,24,128]{2,1,0:T(8,128)}) custom-call(f32[4,24,64,128]{3,2,1,0:T(8,128)} %fusion.66.o_ref, f32[4,24,128]{2,1,0:T(8,128)} %pad_maximum_fusion.4.s_ref), custom_call_target="tpu_custom_call" | custom-call | tf_op jit(solution)/shard_map/home_partials/pallas_call | solution.py:127
  692.1 13.7 %fusion.60 = bf16[48,4096]{1,0:T(8,128)(2,1)S(1)} fusion(bf16[48,4096]{1,0:T(8,128)(2,1)S(1)} %convert_element_type.137, bf16[2,4096,4096]{2,1,0:T(8,128)(2,1)} %param.19, bf16[48,4096]{1,0:T(8,128)(2,1)S(1)} %copy-done.9), kind=kOutput, calls=%fused_computation.44 | convolution fusion | flops 1611202560 | bytes 34734080 | tf_op jit(solution)/shard_map/dot_general | solution.py:423
  710.1 38.8 %fusion.91.clone.5 = bf16[48,14336]{1,0:T(8,128)(2,1)S(1)} fusion(bf16[48,4096]{1,0:T(8,128)(2,1)S(1)} %fusion.60, bf16[2,4096,14336]{2,1,0:T(8,128)(2,1)} %param.20), kind=kOutput, calls=%fused_computation.67.clone.clone.clone.2 | convolution fusion | flops 5643337728 | bytes 119209984 | tf_op jit(solution)/shard_map/dot_general | solution.py:423
  748.9 38.4 %fusion.54 = bf16[48,4096]{1,0:T(8,128)(2,1)S(1)} fusion(bf16[2,14336,4096]{2,1,0:T(8,128)(2,1)} %param.21, bf16[48,4096]{1,0:T(8,128)(2,1)S(1)} %fusion.60, bf16[48,14336]{1,0:T(8,128)(2,1)S(1)} %fusion.91.clone.5), kind=kOutput, calls=%fused_computation.42 | convolution fusion | flops 5637734400 | bytes 119603200 | tf_op jit(solution)/shard_map/dot_general | solution.py:423
  798.5 61.8 %all-to-all-done.3.src_ref = bf16[104,2,32,8,128]{4,3,2,1,0:T(8,128)(2,1)} async-done(((bf16[104,2,32,8,128]{4,3,2,1,0:T(8,128)(2,1)}), bf16[104,2,32,8,128]{4,3,2,1,0:T(8,128)(2,1)}, u32[]{:S(2)}, u32[]{:S(2)}) %all-to-all-start.3) | async-done | bytes 13631520 | tf_op jit(solution)/shard_map/all_to_all | solution.py:393
  (229 shorter events, 131.7 us)
Async XLA Ops:
  7.9 4.3 copy-start.16
  7.9 4.3 copy-start.20
  7.9 5.8 copy-start.10
  7.9 137.7 %all-to-all-start.5 = ((bf16[16,2,32,8,128]{4,3,2,1,0:T(8,128)(2,1)}), bf16[16,2,32,8,128]{4,3,2,1,0:T(8,128)(2,1)}, u32[]{:S(2)}, u32[]{:S(2)}) async-start(bf16[16,2,32,8,128]{4,3,2,1,0:T(8,128)(2,1)} %shard_map.175), calls=%async_computation.5 | async-start | bytes 4194304 | tf_op jit(solution)/shard_map/all_to_all | solution.py:393
  145.6 114.2 %all-to-all-start = ((bf16[48,2,32,8,128]{4,3,2,1,0:T(8,128)(2,1)}), bf16[48,2,32,8,128]{4,3,2,1,0:T(8,128)(2,1)}, u32[]{:S(2)}, u32[]{:S(2)}) async-start(bf16[48,2,32,8,128]{4,3,2,1,0:T(8,128)(2,1)} %shard_map.166), calls=%async_computation | async-start | bytes 12582912 | tf_op jit(solution)/shard_map/all_to_all | solution.py:393
  150.0 9.0 %copy-start.2 = (bf16[8,48,4096]{2,1,0:T(8,128)(2,1)S(1)}, bf16[8,48,4096]{2,1,0:T(8,128)(2,1)}, u32[]{:S(2)}) copy-start(bf16[8,48,4096]{2,1,0:T(8,128)(2,1)} %gather_rows.2) | copy-start | bytes 9437188
  167.2 88.4 %copy-start.14 = (pred[2,2]{1,0:T(4,128)(4,1)}, pred[2,2]{1,0:T(4,128)(4,1)S(1)}, u32[]{:S(2)}) copy-start(pred[2,2]{1,0:T(4,128)(4,1)S(1)} %iota_compare_fusion.14) | copy-start | bytes 16
  168.1 6.3 copy-start.7
  259.8 4.1 copy-start.6
  259.8 98.1 %all-to-all-start.2 = ((bf16[64,2,32,8,128]{4,3,2,1,0:T(8,128)(2,1)}), bf16[64,2,32,8,128]{4,3,2,1,0:T(8,128)(2,1)}, u32[]{:S(2)}, u32[]{:S(2)}) async-start(bf16[64,2,32,8,128]{4,3,2,1,0:T(8,128)(2,1)} %shard_map.168), calls=%async_computation.2 | async-start | bytes 16777216 | tf_op jit(solution)/shard_map/all_to_all | solution.py:393
  357.9 173.8 %all-to-all-start.4 = ((bf16[72,2,32,8,128]{4,3,2,1,0:T(8,128)(2,1)}), bf16[72,2,32,8,128]{4,3,2,1,0:T(8,128)(2,1)}, u32[]{:S(2)}, u32[]{:S(2)}) async-start(bf16[72,2,32,8,128]{4,3,2,1,0:T(8,128)(2,1)} %shard_map.174), calls=%async_computation.4 | async-start | bytes 18874368 | tf_op jit(solution)/shard_map/all_to_all | solution.py:393
  485.7 9.0 %copy-start.3 = (bf16[8,48,4096]{2,1,0:T(8,128)(2,1)S(1)}, bf16[8,48,4096]{2,1,0:T(8,128)(2,1)}, u32[]{:S(2)}) copy-start(bf16[8,48,4096]{2,1,0:T(8,128)(2,1)} %gather_rows.3) | copy-start | bytes 9437188
  494.7 7.8 copy-start.13
  494.7 8.0 copy-start.22
  494.7 8.2 copy-start.21
  531.8 3.9 copy-start.1
  531.8 173.9 %all-to-all-start.1 = ((bf16[80,2,32,8,128]{4,3,2,1,0:T(8,128)(2,1)}), bf16[80,2,32,8,128]{4,3,2,1,0:T(8,128)(2,1)}, u32[]{:S(2)}, u32[]{:S(2)}) async-start(bf16[80,2,32,8,128]{4,3,2,1,0:T(8,128)(2,1)} %shard_map.167), calls=%async_computation.1 | async-start | bytes 20971520 | tf_op jit(solution)/shard_map/all_to_all | solution.py:393
  584.2 6.2 copy-start.8
  705.7 154.6 %all-to-all-start.3 = ((bf16[104,2,32,8,128]{4,3,2,1,0:T(8,128)(2,1)}), bf16[104,2,32,8,128]{4,3,2,1,0:T(8,128)(2,1)}, u32[]{:S(2)}, u32[]{:S(2)}) async-start(bf16[104,2,32,8,128]{4,3,2,1,0:T(8,128)(2,1)} %shard_map.173), calls=%async_computation.3 | async-start | bytes 27262976 | tf_op jit(solution)/shard_map/all_to_all | solution.py:393
  748.8 39.8 %copy-start.23 = (s32[192]{0:T(256)S(1)}, s32[192]{0:T(256)}, u32[]{:S(2)}) copy-start(s32[192]{0:T(256)} %param.27) | copy-start | bytes 2308
  748.9 39.9 %copy-start.17 = (s32[1,1,288]{2,1,0:T(1,128)S(1)}, s32[1,1,288]{2,1,0:T(1,128)}, u32[]{:S(2)}) copy-start(s32[1,1,288]{2,1,0:T(1,128)} %stack.144) | copy-start | bytes 3460
  748.9 39.9 %copy-start.18 = (s32[1,1,288]{2,1,0:T(1,128)S(1)}, s32[1,1,288]{2,1,0:T(1,128)}, u32[]{:S(2)}) copy-start(s32[1,1,288]{2,1,0:T(1,128)} %stack.145) | copy-start | bytes 3460
  748.9 39.9 %copy-start.19 = (s32[1,1,288]{2,1,0:T(1,128)S(1)}, s32[1,1,288]{2,1,0:T(1,128)}, u32[]{:S(2)}) copy-start(s32[1,1,288]{2,1,0:T(1,128)} %stack.146) | copy-start | bytes 3460
  748.9 39.9 %copy-start.24 = (s32[4]{0:T(128)S(1)}, s32[4]{0:T(128)}, u32[]{:S(2)}) copy-start(s32[4]{0:T(128)} %pad.9.clone) | copy-start | bytes 52
  (7 other events, 18.0 us)
